TPU v7x, 256 devices: a whole 4x4x8 slice. The times are simulated.
256 devices in a mesh: sub: 8 (over y_lo, x), col: 16 (over z, core), grp: 2 (over y_hi).
Axes of the slice: x: 4, y: 4 (y_hi: 2, y_lo: 2; y = y_hi * 2 + y_lo), z: 8, core: 2. Of those that a mesh axis runs over, the one named last changes fastest.
Arguments:
- first_rhs: float32 [8, 640, 2048], P('sub', None, 'col'), may hold values from -6 to 6
- innovations: float32 [8, 1024, 640], P('sub', 'col'), may hold values from -6 to 6
- start_mult: float32 [8, 640, 2048], P('sub', None, 'col'), may hold values from -4 to 4
- trajectory: bfloat16 [8, 640, 2048], P('sub', None, 'col'), may hold values from -6 to 6
- weight_in: float32 [4096, 640], P('grp'), may hold values from -0.25 to 0.25
- weight_out: float32 [640, 4096], P(None, 'grp'), may hold values from -0.09375 to 0.09375
- vertical_modes: float32 [640, 640], P('grp'), may hold values from -0.25 to 0.25
- length_scale: float32 [640], replicated, may hold values from 2 to 16
- band_limit: int32 [640], replicated, may hold values from 1 to 128
- obs_col: int32 [8, 1024], P('sub', 'col'), may hold values from 0 to 2047, as said below
- obs_count: int32 [8, 16], P('sub', 'col'), may hold values from 1 to 64
- obs_var: float32 [8, 1024], P('sub', 'col'), may hold values from 0.25 to 4
Outputs:
- multiplier: float32 [8, 640, 2048], P('sub', None, 'col')
- obs_multiplier: float32 [8, 1024, 640], P('sub', 'col')
- increment: float32 [8, 640, 2048], P('sub', None, 'col')
Inputs may be any that keep to these rules, and one draw needn't show every extreme that they name: `obs_col`: slot j of a subwindow observes a column of shard j // 64: a column from (j // 64) * 128 to (j // 64 + 1) * 128 - 1.
All inputs are finite; a program needn't handle non-finite values.
Results may differ from a plain program's by a relative error of at most 0.0003.
Values sent between devices are 32-bit elements; how exact they have to be, the bound alone decides.
A program may use at most 128 MiB of HBM per device.

v0:
```python
import functools
import math

import jax
import jax.numpy as jnp
from jax import lax
from jax.sharding import Mesh
from jax.sharding import PartitionSpec as P

KW = 128
ITERS = 2
COL = ("col_0", "col_1")
SUB = ("sub_0", "sub_1")
SUB_COL = ("sub_0", "sub_1", "col_0", "col_1")


HIGH = lax.Precision.HIGHEST


def sent_to_all(array, axis):
    length = lax.axis_size(axis)
    return lax.all_to_all(
        jnp.broadcast_to(array[None], (length, *array.shape)), axis, 0, 0, tiled=True
    )


def taken_together(array, axis):
    return sent_to_all(array, axis).sum(axis=0)


def passed_along(block, axis, distance):
    devices = range(lax.axis_size(axis))
    route = [(i - distance, i) for i in devices if i - distance in devices]
    return lax.ppermute(block, axis, route)


def over_axes(array, axes):
    return functools.reduce(lax.psum, axes, array)


def product(left, right):
    return jnp.dot(left, right, precision=HIGH, preferred_element_type=jnp.float32)


def product_first(left, right):
    return lax.dot_general(
        left, right, (((0,), (0,)), ((), ())), precision=HIGH, preferred_element_type=jnp.float32
    )


def product_last(left, right):
    return lax.dot_general(
        left, right, (((1,), (1,)), ((), ())), precision=HIGH, preferred_element_type=jnp.float32
    )


def spectral_table(columns, count, total):
    waves = jnp.arange(count, dtype=jnp.int32)
    phase = columns[:, None] * waves[None, :] % total
    angle = 2.0 * math.pi / total * phase.astype(jnp.float32)
    return jnp.concatenate([jnp.cos(angle), jnp.sin(angle)], axis=1)


def spectrum(scales, limits, total, count):
    waves = jnp.arange(count, dtype=jnp.int32)
    wavef = waves.astype(jnp.float32)
    decay = jnp.exp(-0.5 * (2.0 * math.pi * wavef[None, :] * scales[:, None] / total) ** 2)
    factor = jnp.where(waves == 0, 1.0, 2.0).astype(jnp.float32) / total
    keep = (waves[None, :] < limits[:, None]).astype(jnp.float32)
    values = decay * factor[None, :] * keep
    return jnp.concatenate([values, values], axis=1)


def on_device(
    first_rhs,
    innovations,
    start_mult,
    trajectory,
    weight_in,
    weight_out,
    vertical_modes,
    length_scale,
    band_limit,
    obs_col,
    obs_count,
    obs_var,
):
    first_rhs = first_rhs[0]
    innovations = innovations[0]
    start_mult = start_mult[0]
    obs_var = obs_var[0]
    width = first_rhs.shape[1]
    shard_count = lax.axis_size(COL)
    column_index = lax.axis_index(COL)
    group_index = lax.axis_index("grp")
    total_cols = width * shard_count
    half_modes = vertical_modes.shape[0]
    owned_modes = half_modes // shard_count
    slopes = 1.0 - jnp.tanh(product(weight_in, trajectory[0].astype(jnp.float32))) ** 2

    def adjoint(field):
        partial_sum = product_first(weight_in, slopes * product_first(weight_out, field))
        return field + taken_together(partial_sum, "grp")

    def apply_upper(field):
        return field - adjoint(passed_along(field, SUB, -1))

    first_mode = group_index * half_modes + column_index * owned_modes
    owned_scales = lax.dynamic_slice_in_dim(length_scale, first_mode, owned_modes, 0)
    owned_limits = lax.dynamic_slice_in_dim(band_limit, first_mode, owned_modes, 0)
    owned_spec = spectrum(owned_scales, owned_limits, total_cols, KW)

    def covariance(field):
        amplitudes = product(vertical_modes, field)
        owned = lax.all_to_all(amplitudes, COL, split_axis=0, concat_axis=1, tiled=True)
        table = spectral_table(jnp.arange(total_cols, dtype=jnp.int32), KW, total_cols)
        coeffs = product(owned, table) * owned_spec
        back = product_last(coeffs, table)
        returned = lax.all_to_all(back, COL, split_axis=1, concat_axis=0, tiled=True)
        partial_sum = product_first(vertical_modes, returned)
        return taken_together(partial_sum, "grp")

    def running(field, later):
        every = lax.all_gather(field[None], SUB, axis=0, tiled=True)
        position = jnp.arange(every.shape[0], dtype=jnp.int32)
        own_index = lax.axis_index(SUB)
        if later:
            keep = (position >= own_index).astype(jnp.float32)
        else:
            keep = (position <= own_index).astype(jnp.float32)
        return jnp.sum(every * keep[:, None, None], axis=0)

    local_cols = obs_col[0] - column_index * width
    slot_ids = jnp.arange(local_cols.shape[0], dtype=jnp.int32)
    live = (slot_ids < obs_count[0, 0]).astype(jnp.float32)
    pick = (jnp.arange(width, dtype=jnp.int32)[:, None] == local_cols[None, :]).astype(
        jnp.float32
    ) * live[None, :]
    multiplier = start_mult
    obs_multiplier = jnp.zeros_like(innovations)
    increment = jnp.zeros_like(start_mult)
    res_mult = first_rhs - covariance(start_mult)
    res_obs = innovations
    res_state = -apply_upper(start_mult)
    for sweep in range(ITERS):
        dir_mult = running(res_state, True)
        cov_mult = covariance(dir_mult)
        dir_state = running(res_mult - cov_mult, False)
        dir_obs = res_obs / obs_var[:, None]
        tangent_partial_sum = product(weight_out, slopes * product(weight_in, dir_state))
        image_mult = cov_mult + (
            dir_state - passed_along(dir_state + taken_together(tangent_partial_sum, "grp"), SUB, 1)
        )
        image_obs = obs_var[:, None] * dir_obs + lax.dot_general(
            pick,
            dir_state,
            (((0,), (1,)), ((), ())),
            precision=HIGH,
            preferred_element_type=jnp.float32,
        )
        image_state = apply_upper(dir_mult) + lax.dot_general(
            dir_obs,
            pick,
            (((0,), (1,)), ((), ())),
            precision=HIGH,
            preferred_element_type=jnp.float32,
        )
        upper_local = (
            jnp.sum(image_mult * res_mult)
            + jnp.sum(image_obs * res_obs)
            + jnp.sum(image_state * res_state)
        )
        lower_local = (
            jnp.sum(image_mult * image_mult)
            + jnp.sum(image_obs * image_obs)
            + jnp.sum(image_state * image_state)
        )
        upper, lower = (over_axes(upper_local, SUB_COL), over_axes(lower_local, SUB_COL))
        alpha = upper / lower
        multiplier = multiplier + alpha * dir_mult
        obs_multiplier = obs_multiplier + alpha * dir_obs
        increment = increment + alpha * dir_state
        res_mult = res_mult - alpha * image_mult
        res_obs = res_obs - alpha * image_obs
        res_state = res_state - alpha * image_state
    return (multiplier[None], obs_multiplier[None], increment[None])


def solution(mesh):
    torus = Mesh(
        mesh.devices.reshape(2, 4, 8, 2, mesh.shape["grp"]),
        ("sub_0", "sub_1", "col_0", "col_1", "grp"),
    )
    in_specs = (
        P(SUB, None, COL),
        P(SUB, COL, None),
        P(SUB, None, COL),
        P(SUB, None, COL),
        P("grp", None),
        P(None, "grp"),
        P("grp", None),
        P(),
        P(),
        P(SUB, COL),
        P(SUB, COL),
        P(SUB, COL),
    )
    out_specs = (P(SUB, None, COL), P(SUB, COL, None), P(SUB, None, COL))
    return jax.shard_map(
        on_device, mesh=torus, in_specs=in_specs, out_specs=out_specs, check_vma=False
    )
```

profile of v0, /device:TPU:1, one launch (start us, length us, event | category | flops | bytes accessed | tf_op | source)
XLA Modules:
  0.0 549.7 jit_solution(3880028823583145042)
XLA Ops:
  8.8 5.9 %fusion.5 = f32[2048,128]{1,0:T(8,128)} fusion(f32[2048,640]{1,0:T(8,128)} %param.16, bf16[1,640,128]{2,1,0:T(8,128)(2,1)S(1)} %copy-done), kind=kOutput, calls=%fused_computation.15 | convolution fusion | flops 2013790208 | bytes 6455296 | tf_op jit(solution)/shard_map/dot_general | solution.py:42
  14.8 2.3 collective-permute-done
  17.1 10.0 %convolution_multiply_fusion = f32[2048,128]{1,0:T(8,128)S(1)} fusion(f32[2048,128]{1,0:T(8,128)} %fusion.5, f32[640,2048]{1,0:T(8,128)S(1)} %copy-done.1, f32[640,128]{1,0:T(8,128)S(1)} %collective-permute-done), kind=kOutput, calls=%fused_computation.12 | convolution fusion | flops 2013528064 | bytes 7667712 | tf_op jit(solution)/shard_map/dot_general | solution.py:46
  27.1 3.7 convolution_bitcast_fusion.11
  31.1 15.2 %all_to_all.151 = f32[2,640,128]{2,1,0:T(8,128)S(1)} all-to-all(f32[2,640,128]{2,1,0:T(8,128)S(1)} %broadcast_in_dim.32), channel_id=1, replica_groups=mesh['sub_0'=2,'sub_1'=4,'col_0'=8,'col_1'=2,'grp'=2] {'grp'}, dimensions={0} | all-to-all | bytes 1310720 | tf_op jit(solution)/shard_map/all_to_all | solution.py:22
  48.9 11.1 %all-to-all-start.4 = ((f32[16,20,128]{2,1,0:T(8,128)}), f32[16,20,128]{2,1,0:T(8,128)S(1)}, u32[]{:S(2)}, u32[]{:S(2)}) async-start(f32[16,20,128]{2,1,0:T(8,128)} %fusion.14), calls=%async_computation.4 | async-start | bytes 393216 | tf_op jit(solution)/shard_map/all_to_all | solution.py:115
  61.7 4.1 fusion.12
  65.8 4.5 all-to-all-done.4
  70.4 21.5 %all-gather.10.cloned.1.call-done = f32[5120,128]{1,0:T(8,128)} async-done(((f32[640,128]{1,0:T(8,128)}), f32[5120,128]{1,0:T(8,128)}) %all-gather.10.cloned.1.call-update) | async-done | bytes 2621456 | tf_op jit(solution)/shard_map/all_gather | solution.py:124
  92.0 2.0 multiply_reduce_fusion.3
  96.2 11.5 %all-to-all-start.1 = ((f32[16,20,128]{2,1,0:T(8,128)}), f32[16,20,128]{2,1,0:T(8,128)S(1)}, u32[]{:S(2)}, u32[]{:S(2)}) async-start(f32[16,20,128]{2,1,0:T(8,128)} %all_to_all.107), calls=%async_computation.1 | async-start | bytes 393216 | tf_op jit(solution)/shard_map/all_to_all | solution.py:115
  111.3 6.5 %all-to-all-done.1 = f32[16,20,128]{2,1,0:T(8,128)S(1)} async-done(((f32[16,20,128]{2,1,0:T(8,128)}), f32[16,20,128]{2,1,0:T(8,128)S(1)}, u32[]{:S(2)}, u32[]{:S(2)}) %all-to-all-start.1) | async-done | bytes 163872 | tf_op jit(solution)/shard_map/all_to_all | solution.py:115
  118.5 3.4 all-to-all-start.5
  126.6 5.2 all-to-all-done.5
  131.7 3.4 all-to-all-start.2
  135.8 2.5 convolution_bitcast_fusion.5
  140.2 5.2 all-to-all-done.2
  147.3 4.3 all-to-all-start.6
  154.3 8.6 %all-to-all-done.6 = f32[2,640,128]{2,1,0:T(8,128)} async-done(((f32[2,640,128]{2,1,0:T(8,128)}), f32[2,640,128]{2,1,0:T(8,128)}, u32[]{:S(2)}, u32[]{:S(2)}) %all-to-all-start.6) | async-done | bytes 655392 | tf_op jit(solution)/shard_map/all_to_all | solution.py:22
  163.8 4.3 all-to-all-start.3
  168.1 1.9 reduce_sum.223
  170.0 8.5 %all-to-all-done.3 = f32[2,640,128]{2,1,0:T(8,128)} async-done(((f32[2,640,128]{2,1,0:T(8,128)}), f32[2,640,128]{2,1,0:T(8,128)}, u32[]{:S(2)}, u32[]{:S(2)}) %all-to-all-start.3) | async-done | bytes 655392 | tf_op jit(solution)/shard_map/all_to_all | solution.py:22
  178.5 2.0 reduce_sum.222
  180.5 2.0 bitcast_subtract_fusion.1
  184.9 10.0 %collective-permute-done.2 = f32[640,128]{1,0:T(8,128)} collective-permute-done((f32[640,128]{1,0:T(8,128)}, f32[640,128]{1,0:T(8,128)}, u32[]{:S(2)}, u32[]{:S(2)}) %collective-permute-start.2) | collective-permute-done | bytes 327712 | tf_op jit(solution)/shard_map/ppermute | solution.py:34
  194.9 10.8 %fusion.2 = f32[2048,128]{1,0:T(8,128)S(1)} fusion(f32[2048,128]{1,0:T(8,128)} %fusion.5, f32[640,128]{1,0:T(8,128)} %collective-permute-done.2, f32[640,2048]{1,0:T(8,128)} %param.17), kind=kOutput, calls=%fused_computation.9 | convolution fusion | flops 2013528064 | bytes 7667712 | tf_op jit(solution)/shard_map/dot_general | solution.py:46
  205.7 4.3 convolution_bitcast_fusion.9
  212.1 4.4 all-to-all-start.8
  216.5 3.3 all-gather.8.cloned.1.call-done
  219.8 2.2 multiply_reduce_fusion.2
  222.0 6.8 %fusion.3 = f32[2048,128]{1,0:T(8,128)S(1)} fusion(f32[2048,128]{1,0:T(8,128)} %fusion.5, f32[640,128]{1,0:T(8,128)S(1)} %multiply_reduce_fusion.2, f32[2048,640]{1,0:T(8,128)} %param.16), kind=kOutput, calls=%fused_computation.11 | convolution fusion | flops 2013528064 | bytes 7667712 | tf_op jit(solution)/shard_map/dot_general | solution.py:42
  228.8 6.1 %convolution_bitcast_fusion.10 = f32[640,128]{0,1:T(8,128)S(1)} fusion(f32[2048,128]{1,0:T(8,128)S(1)} %fusion.3, f32[640,2048]{1,0:T(8,128)S(1)} %bitcast.162), kind=kOutput, calls=%fused_computation.26 | convolution fusion | flops 2013265920 | bytes 6619136 | tf_op jit(solution)/shard_map/dot_general | solution.py:42
  235.9 1.9 broadcast_in_dim.38
  237.8 4.3 all-to-all-start.7
  242.1 1.9 reduce_sum.230
  244.0 5.8 %all-to-all-done.7 = f32[2,640,128]{2,1,0:T(8,128)} async-done(((f32[2,640,128]{2,1,0:T(8,128)}), f32[2,640,128]{2,1,0:T(8,128)}, u32[]{:S(2)}, u32[]{:S(2)}) %all-to-all-start.7) | async-done | bytes 655392 | tf_op jit(solution)/shard_map/all_to_all | solution.py:22
  249.8 1.9 reduce_sum.227
  252.8 3.3 collective-permute-start.1
  256.1 3.2 multiply_reduce_fusion.8
  266.5 6.3 %all-reduce.7 = (f32[]{:T(128)}, f32[]{:T(128)}) all-reduce(f32[]{:T(128)S(6)} %add.153, f32[]{:T(128)S(6)} %add.155), channel_id=1, replica_groups=mesh['sub_0'=2,'sub_1'=4,'col_0'=8,'col_1'=2,'grp'=2] {'sub_0'}, use_global_device_ids=true, to_apply=%region_10.11 | all-reduce | flops 2 | bytes 16 | tf_op jit(solution)/shard_map/psum | solution.py:38
  272.8 7.7 %all-reduce.3 = (f32[]{:T(128)}, f32[]{:T(128)}) all-reduce(f32[]{:T(128)} %get-tuple-element.29, f32[]{:T(128)} %get-tuple-element.30), channel_id=1, replica_groups=mesh['sub_0'=2,'sub_1'=4,'col_0'=8,'col_1'=2,'grp'=2] {'sub_1'}, use_global_device_ids=true, to_apply=%region_11.12 | all-reduce | flops 2 | bytes 16 | tf_op jit(solution)/shard_map/psum | solution.py:38
  280.5 11.4 %all-reduce.1 = (f32[]{:T(128)}, f32[]{:T(128)}) all-reduce(f32[]{:T(128)} %get-tuple-element.21, f32[]{:T(128)} %get-tuple-element.22), channel_id=1, replica_groups=mesh['sub_0'=2,'sub_1'=4,'col_0'=8,'col_1'=2,'grp'=2] {'col_0'}, use_global_device_ids=true, to_apply=%region_12.13 | all-reduce | flops 2 | bytes 16 | tf_op jit(solution)/shard_map/psum | solution.py:38
  291.8 16.2 %all-reduce.5 = (f32[]{:T(128)}, f32[]{:T(128)}) all-reduce(f32[]{:T(128)} %get-tuple-element.17, f32[]{:T(128)} %get-tuple-element.18), channel_id=1, replica_groups=mesh['sub_0'=2,'sub_1'=4,'col_0'=8,'col_1'=2,'grp'=2] {'col_1'}, use_global_device_ids=true, to_apply=%region_13.14 | all-reduce | flops 2 | bytes 16 | tf_op jit(solution)/shard_map/psum | solution.py:38
  311.3 34.7 %all-gather.12.cloned.1.call-done = f32[5120,128]{1,0:T(8,128)} async-done(((f32[640,128]{1,0:T(8,128)}), f32[5120,128]{1,0:T(8,128)}) %all-gather.12.cloned.1.call-update) | async-done | bytes 2621456 | tf_op jit(solution)/shard_map/all_gather | solution.py:124
  346.0 2.0 multiply_reduce_fusion.1
  351.2 21.4 %all_to_all.152 = f32[16,20,128]{2,1,0:T(8,128)S(1)} all-to-all(f32[16,20,128]{2,1,0:T(8,128)S(1)} %all_to_all.126), channel_id=1, replica_groups=mesh['sub_0'=2,'sub_1'=4,'col_0'=8,'col_1'=2,'grp'=2] {'col_0','col_1'}, dimensions={0} | all-to-all | bytes 327680 | tf_op jit(solution)/shard_map/all_to_all | solution.py:115
  375.6 13.0 %all_to_all.153 = f32[20,16,128]{2,0,1:T(8,128)S(1)} all-to-all(f32[20,16,128]{2,0,1:T(8,128)S(1)} %copy.67), channel_id=1, replica_groups=mesh['sub_0'=2,'sub_1'=4,'col_0'=8,'col_1'=2,'grp'=2] {'col_0','col_1'}, dimensions={1} | all-to-all | bytes 327680 | tf_op jit(solution)/shard_map/all_to_all | solution.py:119
  389.7 14.6 %all_to_all.154 = f32[2,640,128]{2,1,0:T(8,128)S(1)} all-to-all(f32[2,640,128]{2,1,0:T(8,128)S(1)} %broadcast_in_dim.41), channel_id=1, replica_groups=mesh['sub_0'=2,'sub_1'=4,'col_0'=8,'col_1'=2,'grp'=2] {'grp'}, dimensions={0} | all-to-all | bytes 1310720 | tf_op jit(solution)/shard_map/all_to_all | solution.py:22
  406.6 12.2 %collective-permute-done.4 = f32[640,128]{1,0:T(8,128)S(1)} collective-permute-done((f32[640,128]{1,0:T(8,128)S(1)}, f32[640,128]{1,0:T(8,128)S(1)}, u32[]{:S(2)}, u32[]{:S(2)}) %collective-permute-start.4) | collective-permute-done | bytes 327712 | tf_op jit(solution)/shard_map/ppermute | solution.py:34
  419.5 10.5 %fusion = f32[2048,128]{1,0:T(8,128)S(1)} fusion(f32[2048,128]{1,0:T(8,128)} %fusion.5, f32[640,128]{1,0:T(8,128)S(1)} %collective-permute-done.4, f32[640,2048]{1,0:T(8,128)} %param.17), kind=kOutput, calls=%fused_computation.5 | convolution fusion | flops 2013528064 | bytes 7667712 | tf_op jit(solution)/shard_map/dot_general | solution.py:46
  430.0 12.3 %all-gather.14.cloned.1.call-done = f32[5120,128]{1,0:T(8,128)} async-done(((f32[640,128]{1,0:T(8,128)}), f32[5120,128]{1,0:T(8,128)}) %all-gather.14.cloned.1.call-update) | async-done | bytes 2621456 | tf_op jit(solution)/shard_map/all_gather | solution.py:124
  442.3 2.2 multiply_reduce_fusion
  444.4 7.0 %fusion.1 = f32[2048,128]{1,0:T(8,128)S(1)} fusion(f32[2048,128]{1,0:T(8,128)} %fusion.5, f32[640,128]{1,0:T(8,128)S(1)} %multiply_reduce_fusion, f32[2048,640]{1,0:T(8,128)} %param.16), kind=kOutput, calls=%fused_computation.7 | convolution fusion | flops 2013528064 | bytes 7667712 | tf_op jit(solution)/shard_map/dot_general | solution.py:42
  451.4 6.1 %convolution_bitcast_fusion.8 = f32[640,128]{0,1:T(8,128)S(1)} fusion(f32[2048,128]{1,0:T(8,128)S(1)} %fusion.1, f32[640,2048]{1,0:T(8,128)S(1)} %bitcast.164), kind=kOutput, calls=%fused_computation.24 | convolution fusion | flops 2013265920 | bytes 6619136 | tf_op jit(solution)/shard_map/dot_general | solution.py:42
  458.6 3.5 all-to-all-start.12
  462.2 6.6 %convolution_bitcast_fusion.7 = f32[640,128]{0,1:T(8,128)} fusion(f32[2048,128]{1,0:T(8,128)S(1)} %fusion, f32[2048,640]{1,0:T(8,128)} %param.16), kind=kOutput, calls=%fused_computation.23 | convolution fusion | flops 2013265920 | bytes 6619136 | tf_op jit(solution)/shard_map/dot_general | solution.py:46
  470.8 4.4 all-to-all-start.13
  476.0 4.2 collective-permute-start.3
  480.3 2.7 all-to-all-done.13
  484.1 2.3 multiply_reduce_fusion.4
  493.3 4.8 all-reduce.6
  498.1 9.3 %all-reduce.2 = (f32[]{:T(128)}, f32[]{:T(128)}) all-reduce(f32[]{:T(128)} %get-tuple-element.27, f32[]{:T(128)} %get-tuple-element.28), channel_id=1, replica_groups=mesh['sub_0'=2,'sub_1'=4,'col_0'=8,'col_1'=2,'grp'=2] {'sub_1'}, use_global_device_ids=true, to_apply=%region_30.31 | all-reduce | flops 2 | bytes 16 | tf_op jit(solution)/shard_map/psum | solution.py:38
  507.3 11.5 %all-reduce = (f32[]{:T(128)}, f32[]{:T(128)}) all-reduce(f32[]{:T(128)} %get-tuple-element.19, f32[]{:T(128)} %get-tuple-element.20), channel_id=1, replica_groups=mesh['sub_0'=2,'sub_1'=4,'col_0'=8,'col_1'=2,'grp'=2] {'col_0'}, use_global_device_ids=true, to_apply=%region_31.32 | all-reduce | flops 2 | bytes 16 | tf_op jit(solution)/shard_map/psum | solution.py:38
  518.9 20.2 %all-reduce.4 = (f32[]{:T(128)}, f32[]{:T(128)}) all-reduce(f32[]{:T(128)} %get-tuple-element.15, f32[]{:T(128)} %get-tuple-element.16), channel_id=1, replica_groups=mesh['sub_0'=2,'sub_1'=4,'col_0'=8,'col_1'=2,'grp'=2] {'col_1'}, use_global_device_ids=true, to_apply=%region_32.33 | all-reduce | flops 2 | bytes 16 | tf_op jit(solution)/shard_map/psum | solution.py:38
  (164 shorter events, 56.9 us)
Async XLA Ops:
  7.2 1.6 copy-start
  7.2 84.8 %all-gather.10.cloned.1.call-start = ((), (), s32[]{:S(2)}) async-start(), calls=%async_computation.15 | async-start | bytes 2949120 | tf_op jit(solution)/shard_map/all_gather | solution.py:124
  7.2 9.9 %copy-start.1 = (f32[640,2048]{1,0:T(8,128)S(1)}, f32[640,2048]{1,0:T(8,128)}, u32[]{:S(2)}) copy-start(f32[640,2048]{1,0:T(8,128)} %param.17) | copy-start | bytes 15728644
  7.2 9.8 %collective-permute-start = (f32[640,128]{1,0:T(8,128)}, f32[640,128]{1,0:T(8,128)S(1)}, u32[]{:S(2)}, u32[]{:S(2)}) collective-permute-start(f32[640,128]{1,0:T(8,128)} %bitcast.165), channel_id=1, source_target_pairs={{32,0},{64,32},{96,64},{128,96},{160,128},{192,160},{224,192},{33,... | collective-permute-start | bytes 983048 | tf_op jit(solution)/shard_map/ppermute | solution.py:34
  8.8 18.3 %slice-start = ((s8[5242880]{0:T(1024)(128)(4,1)}), s8[4194304]{0:T(1024)(128)(4,1)S(1)}, s32[]{:S(2)}) async-start(s8[5242880]{0:T(1024)(128)(4,1)} %bitcast.157), calls=%async_computation.18 | async-start | bytes 8388608
  14.8 12.4 %slice-start.1 = ((s8[5242880]{0:T(1024)(128)(4,1)}), s8[1048576]{0:T(1024)(128)(4,1)S(1)}, s32[]{:S(2)}) async-start(s8[5242880]{0:T(1024)(128)(4,1)} %bitcast.157), calls=%async_computation.19 | async-start | bytes 2097152
  30.9 15.5 %copy-start.18 = (f32[1,640,128]{2,1,0:T(8,128)S(1)}, f32[1,640,128]{2,1,0:T(8,128)}, u32[]{:S(2)}) copy-start(f32[1,640,128]{2,1,0:T(8,128)} %param.14) | copy-start | bytes 983044
  31.1 16.1 %copy-start.2 = (f32[320,640]{1,0:T(8,128)S(1)}, f32[320,640]{1,0:T(8,128)}, u32[]{:S(2)}) copy-start(f32[320,640]{1,0:T(8,128)} %param.18) | copy-start | bytes 2457604
  48.9 21.3 %all-to-all-start.4 = ((f32[16,20,128]{2,1,0:T(8,128)}), f32[16,20,128]{2,1,0:T(8,128)S(1)}, u32[]{:S(2)}, u32[]{:S(2)}) async-start(f32[16,20,128]{2,1,0:T(8,128)} %fusion.14), calls=%async_computation.4 | async-start | bytes 393216 | tf_op jit(solution)/shard_map/all_to_all | solution.py:115
  94.0 0.7 copy-start.7
  96.2 21.6 %all-to-all-start.1 = ((f32[16,20,128]{2,1,0:T(8,128)}), f32[16,20,128]{2,1,0:T(8,128)S(1)}, u32[]{:S(2)}, u32[]{:S(2)}) async-start(f32[16,20,128]{2,1,0:T(8,128)} %all_to_all.107), calls=%async_computation.1 | async-start | bytes 393216 | tf_op jit(solution)/shard_map/all_to_all | solution.py:115
  117.9 0.7 copy-start.23
  118.5 13.2 %all-to-all-start.5 = ((f32[20,16,128]{2,0,1:T(8,128)}), f32[20,16,128]{2,0,1:T(8,128)S(1)}, u32[]{:S(2)}, u32[]{:S(2)}) async-start(f32[20,16,128]{2,0,1:T(8,128)} %copy.60), calls=%async_computation.5 | async-start | bytes 393216 | tf_op jit(solution)/shard_map/all_to_all | solution.py:119
  131.7 13.7 %all-to-all-start.2 = ((f32[20,16,128]{2,0,1:T(8,128)}), f32[20,16,128]{2,0,1:T(8,128)S(1)}, u32[]{:S(2)}, u32[]{:S(2)}) async-start(f32[20,16,128]{2,0,1:T(8,128)} %copy.57), calls=%async_computation.2 | async-start | bytes 393216 | tf_op jit(solution)/shard_map/all_to_all | solution.py:119
  147.3 15.6 %all-to-all-start.6 = ((f32[2,640,128]{2,1,0:T(8,128)}), f32[2,640,128]{2,1,0:T(8,128)}, u32[]{:S(2)}, u32[]{:S(2)}) async-start(f32[2,640,128]{2,1,0:T(8,128)} %broadcast_in_dim.37), calls=%async_computation.6 | async-start | bytes 1310720 | tf_op jit(solution)/shard_map/all_to_all | solution.py:22
  163.8 14.8 %all-to-all-start.3 = ((f32[2,640,128]{2,1,0:T(8,128)}), f32[2,640,128]{2,1,0:T(8,128)}, u32[]{:S(2)}, u32[]{:S(2)}) async-start(f32[2,640,128]{2,1,0:T(8,128)} %broadcast_in_dim.36), calls=%async_computation.3 | async-start | bytes 1310720 | tf_op jit(solution)/shard_map/all_to_all | solution.py:22
  168.0 51.8 %all-gather.8.cloned.1.call-start = ((), (), s32[]{:S(2)}) async-start(), calls=%async_computation.14 | async-start | bytes 2949120 | tf_op jit(solution)/shard_map/all_gather | solution.py:124
  178.5 27.2 %slice-start.2 = ((s8[5242880]{0:T(1024)(128)(4,1)}), s8[1048576]{0:T(1024)(128)(4,1)S(1)}, s32[]{:S(2)}) async-start(s8[5242880]{0:T(1024)(128)(4,1)} %bitcast.159), calls=%async_computation.20 | async-start | bytes 2097152
  182.5 12.4 %collective-permute-start.2 = (f32[640,128]{1,0:T(8,128)}, f32[640,128]{1,0:T(8,128)}, u32[]{:S(2)}, u32[]{:S(2)}) collective-permute-start(f32[640,128]{1,0:T(8,128)} %copy-done.7), channel_id=1, source_target_pairs={{32,0},{64,32},{96,64},{128,96},{160,128},{192,160},{224,192},{33,... | collective-permute-start | bytes 983048 | tf_op jit(solution)/shard_map/ppermute | solution.py:34
  184.9 20.9 %slice-start.3 = ((s8[5242880]{0:T(1024)(128)(4,1)}), s8[4194304]{0:T(1024)(128)(4,1)S(1)}, s32[]{:S(2)}) async-start(s8[5242880]{0:T(1024)(128)(4,1)} %bitcast.159), calls=%async_computation.21 | async-start | bytes 8388608
  212.1 23.8 %all-to-all-start.8 = ((f32[2,640,128]{2,1,0:T(8,128)}), f32[2,640,128]{2,1,0:T(8,128)}, u32[]{:S(2)}, u32[]{:S(2)}) async-start(f32[2,640,128]{2,1,0:T(8,128)} %broadcast_in_dim.39), calls=%async_computation.8 | async-start | bytes 1310720 | tf_op jit(solution)/shard_map/all_to_all | solution.py:22
  219.8 9.0 %slice-start.4 = ((s8[5242880]{0:T(1024)(128)(4,1)}), s8[4194304]{0:T(1024)(128)(4,1)S(1)}, s32[]{:S(2)}) async-start(s8[5242880]{0:T(1024)(128)(4,1)} %bitcast.161), calls=%async_computation.22 | async-start | bytes 8388608
  222.0 39.2 %copy-start.4 = (f32[640,128]{1,0:T(8,128)}, f32[640,128]{1,0:T(8,128)S(1)}, u32[]{:S(2)}) copy-start(f32[640,128]{1,0:T(8,128)S(1)} %multiply_reduce_fusion.2) | copy-start | bytes 983044
  222.0 6.8 %slice-start.5 = ((s8[5242880]{0:T(1024)(128)(4,1)}), s8[1048576]{0:T(1024)(128)(4,1)S(1)}, s32[]{:S(2)}) async-start(s8[5242880]{0:T(1024)(128)(4,1)} %bitcast.161), calls=%async_computation.23 | async-start | bytes 2097152
  234.9 7.2 %copy-start.26 = (s32[1,64]{1,0:T(1,128)S(1)}, s32[1,64]{1,0:T(1,128)}, u32[]{:S(2)}) copy-start(s32[1,64]{1,0:T(1,128)} %param.21) | copy-start | bytes 772
  235.8 20.2 %copy-start.6 = (f32[640,128]{1,0:T(8,128)S(1)}, f32[640,128]{1,0:T(8,128)}, u32[]{:S(2)}) copy-start(f32[640,128]{1,0:T(8,128)} %subtract_negate_fusion) | copy-start | bytes 983044
  235.8 20.2 %copy-start.8 = (f32[640,128]{1,0:T(8,128)S(1)}, f32[640,128]{1,0:T(8,128)}, u32[]{:S(2)}) copy-start(f32[640,128]{1,0:T(8,128)} %copy-done.7) | copy-start | bytes 983044
  235.8 20.2 %copy-start.20 = (f32[1,64,640]{2,1,0:T(8,128)S(1)}, f32[1,64,640]{2,1,0:T(8,128)}, u32[]{:S(2)}) copy-start(f32[1,64,640]{2,1,0:T(8,128)} %param.13) | copy-start | bytes 491524
  235.8 20.2 %copy-start.25 = (f32[1,64]{1,0:T(1,128)S(1)}, f32[1,64]{1,0:T(1,128)}, u32[]{:S(2)}) copy-start(f32[1,64]{1,0:T(1,128)} %param.23) | copy-start | bytes 772
  237.8 12.0 %all-to-all-start.7 = ((f32[2,640,128]{2,1,0:T(8,128)}), f32[2,640,128]{2,1,0:T(8,128)}, u32[]{:S(2)}, u32[]{:S(2)}) async-start(f32[2,640,128]{2,1,0:T(8,128)} %broadcast_in_dim.38), calls=%async_computation.7 | async-start | bytes 1310720 | tf_op jit(solution)/shard_map/all_to_all | solution.py:22
  242.1 103.9 %all-gather.12.cloned.1.call-start = ((), (), s32[]{:S(2)}) async-start(), calls=%async_computation.16 | async-start | bytes 2949120 | tf_op jit(solution)/shard_map/all_gather | solution.py:124
  251.7 9.5 %copy-start.10 = (f32[640,128]{1,0:T(8,128)S(1)}, f32[640,128]{1,0:T(8,128)}, u32[]{:S(2)}) copy-start(f32[640,128]{1,0:T(8,128)} %reduce_sum.223) | copy-start | bytes 983044
  251.7 9.5 %copy-start.14 = (f32[640,128]{1,0:T(8,128)S(1)}, f32[640,128]{1,0:T(8,128)}, u32[]{:S(2)}) copy-start(f32[640,128]{1,0:T(8,128)} %reduce_sum.222) | copy-start | bytes 983044
  251.7 9.5 %copy-start.15 = (f32[1,640,128]{2,1,0:T(8,128)S(1)}, f32[1,640,128]{2,1,0:T(8,128)}, u32[]{:S(2)}) copy-start(f32[1,640,128]{2,1,0:T(8,128)} %param.12) | copy-start | bytes 983044
  252.8 8.4 %collective-permute-start.1 = (f32[640,128]{1,0:T(8,128)S(1)}, f32[640,128]{1,0:T(8,128)S(1)}, u32[]{:S(2)}, u32[]{:S(2)}) collective-permute-start(f32[640,128]{1,0:T(8,128)S(1)} %add.147), channel_id=1, source_target_pairs={{0,32},{32,64},{64,96},{96,128},{128,160},{160,192},{192,224},{1,3... | collective-permute-start | bytes 983048 | tf_op jit(solution)/shard_map/ppermute | solution.py:34
  262.7 86.1 %copy-start.3 = (f32[320,640]{1,0:T(8,128)S(1)}, f32[320,640]{1,0:T(8,128)}, u32[]{:S(2)}) copy-start(f32[320,640]{1,0:T(8,128)} %param.18) | copy-start | bytes 2457604
  311.2 131.0 %all-gather.14.cloned.1.call-start = ((), (), s32[]{:S(2)}) async-start(), calls=%async_computation.17 | async-start | bytes 2949120 | tf_op jit(solution)/shard_map/all_gather | solution.py:124
  348.0 0.7 copy-start.12
  388.6 15.7 %copy-start.11 = (f32[640,128]{1,0:T(8,128)S(1)}, f32[640,128]{1,0:T(8,128)}, u32[]{:S(2)}) copy-start(f32[640,128]{1,0:T(8,128)} %reduce_sum.223) | copy-start | bytes 983044
  388.6 15.7 %copy-start.16 = (f32[1,640,128]{2,1,0:T(8,128)S(1)}, f32[1,640,128]{2,1,0:T(8,128)}, u32[]{:S(2)}) copy-start(f32[1,640,128]{2,1,0:T(8,128)} %param.12) | copy-start | bytes 983044
  389.5 14.9 %copy-start.21 = (f32[640,128]{1,0:T(8,128)S(1)}, f32[640,128]{1,0:T(8,128)}, u32[]{:S(2)}) copy-start(f32[640,128]{1,0:T(8,128)} %get-tuple-element.33) | copy-start | bytes 983044
  389.6 15.6 %copy-start.13 = (f32[640,128]{1,0:T(8,128)S(1)}, f32[640,128]{1,0:T(8,128)}, u32[]{:S(2)}) copy-start(f32[640,128]{1,0:T(8,128)} %copy-done.12) | copy-start | bytes 983044
  405.3 13.5 %collective-permute-start.4 = (f32[640,128]{1,0:T(8,128)S(1)}, f32[640,128]{1,0:T(8,128)S(1)}, u32[]{:S(2)}, u32[]{:S(2)}) collective-permute-start(f32[640,128]{1,0:T(8,128)S(1)} %copy-done.13), channel_id=1, source_target_pairs={{32,0},{64,32},{96,64},{128,96},{160,128},{192,160},{224,192},{33,... | collective-permute-start | bytes 983048 | tf_op jit(solution)/shard_map/ppermute | solution.py:34
  418.7 0.7 copy-start.22
  442.3 9.2 %slice-start.6 = ((s8[5242880]{0:T(1024)(128)(4,1)}), s8[4194304]{0:T(1024)(128)(4,1)S(1)}, s32[]{:S(2)}) async-start(s8[5242880]{0:T(1024)(128)(4,1)} %bitcast.163), calls=%async_computation.24 | async-start | bytes 8388608
  444.4 7.0 %slice-start.7 = ((s8[5242880]{0:T(1024)(128)(4,1)}), s8[1048576]{0:T(1024)(128)(4,1)S(1)}, s32[]{:S(2)}) async-start(s8[5242880]{0:T(1024)(128)(4,1)} %bitcast.163), calls=%async_computation.25 | async-start | bytes 2097152
  458.6 11.3 %all-to-all-start.12 = ((f32[2,640,128]{2,1,0:T(8,128)}), f32[2,640,128]{2,1,0:T(8,128)S(1)}, u32[]{:S(2)}, u32[]{:S(2)}) async-start(f32[2,640,128]{2,1,0:T(8,128)} %broadcast_in_dim.43), calls=%async_computation.12 | async-start | bytes 1310720 | tf_op jit(solution)/shard_map/all_to_all | solution.py:22
  468.7 11.4 %copy-start.24 = (f32[64,640]{1,0:T(8,128)S(1)}, f32[64,640]{1,0:T(8,128)}, u32[]{:S(2)}) copy-start(f32[64,640]{1,0:T(8,128)} %get-tuple-element.34) | copy-start | bytes 491524
  470.8 13.3 %copy-start.17 = (f32[640,128]{1,0:T(8,128)S(1)}, f32[640,128]{1,0:T(8,128)}, u32[]{:S(2)}) copy-start(f32[640,128]{1,0:T(8,128)} %multiply_subtract_fusion.1) | copy-start | bytes 983044
  470.8 12.1 %all-to-all-start.13 = ((f32[2,640,128]{2,1,0:T(8,128)}), f32[2,640,128]{2,1,0:T(8,128)}, u32[]{:S(2)}, u32[]{:S(2)}) async-start(f32[2,640,128]{2,1,0:T(8,128)} %broadcast_in_dim.44), calls=%async_computation.13 | async-start | bytes 1310720 | tf_op jit(solution)/shard_map/all_to_all | solution.py:22
  476.0 64.4 %copy-start.5 = (f32[640,128]{1,0:T(8,128)S(1)}, f32[640,128]{1,0:T(8,128)}, u32[]{:S(2)}) copy-start(f32[640,128]{1,0:T(8,128)} %copy-done.4) | copy-start | bytes 983044
  476.0 11.7 %collective-permute-start.3 = (f32[640,128]{1,0:T(8,128)}, f32[640,128]{1,0:T(8,128)}, u32[]{:S(2)}, u32[]{:S(2)}) collective-permute-start(f32[640,128]{1,0:T(8,128)} %add.157), channel_id=1, source_target_pairs={{0,32},{32,64},{64,96},{96,128},{128,160},{160,192},{192,224},{1,3... | collective-permute-start | bytes 983048 | tf_op jit(solution)/shard_map/ppermute | solution.py:34
  480.3 60.9 %copy-start.9 = (f32[640,128]{1,0:T(8,128)S(1)}, f32[640,128]{1,0:T(8,128)}, u32[]{:S(2)}) copy-start(f32[640,128]{1,0:T(8,128)} %copy-done.7) | copy-start | bytes 983044
  480.3 60.9 %copy-start.19 = (f32[1,640,128]{2,1,0:T(8,128)S(1)}, f32[1,640,128]{2,1,0:T(8,128)}, u32[]{:S(2)}) copy-start(f32[1,640,128]{2,1,0:T(8,128)} %param.14) | copy-start | bytes 983044
Sparse Core Ops, SparseCore 0:
  47.3 44.6 all-gather.9
  182.6 37.1 all-gather.7
  311.4 34.5 all-gather.11
  405.4 36.8 all-gather.13
where the time goes:
time: 561 us; the launch traced here: 550 us
  blocking collectives  151 us (27%)
  waiting for transfers between devices  143 us (25%)
  matrix products  104 us (19%)
  starting transfers between devices  66.7 us (12%)
  other arithmetic  34.4 us (6%)
  between operations  26.1 us (5%)
  local copies, waits for them, and re-layouts  24 us (4%)
    psum x8, blocking collectives, over_axes(): return functools.reduce(lax.psum, axes, array)  87.2 us
    all_gather x4, waiting for transfers between devices, running(): every = lax.all_gather(field[None], SUB, axis=0, tiled=True)  71.8 us
    dot_general x9, matrix products, product_first(): lax.dot_general(left, right, (((0,), (0,)), ((), ())), precision=HIGH, pr...  50.9 us
    dot_general x11, matrix products, product(): jnp.dot(left, right, precision=HIGH, preferred_element_type=jnp.float32)  38.7 us
    all_to_all x2, blocking collectives, sent_to_all(): lax.all_to_all(jnp.broadcast_to(array[None], (length, *array.shape)), axi...  29.8 us
    all_to_all x6, waiting for transfers between devices, sent_to_all(): lax.all_to_all(jnp.broadcast_to(array[None], (length, *array.shape)), axi...  25.6 us
    all_to_all x6, starting transfers between devices, sent_to_all(): lax.all_to_all(jnp.broadcast_to(array[None], (length, *array.shape)), axi...  25.1 us
    ppermute x5, waiting for transfers between devices, passed_along(): return lax.ppermute(block, axis, route)  24.5 us
  transfers between devices with their start and end apart: 19, of which 15 were waited for; matrix products, arithmetic and copies ran while one was open for 17% of the time, Pallas kernels for 0%

commit v1 on v0

v1 whole, which is shorter than its diff:
```python
import math
import types

import jax
import jax.numpy as jnp
import numpy as np
from jax import lax
from jax.experimental import pallas as pl
from jax.experimental.pallas import tpu as pltpu
from jax.sharding import PartitionSpec as P

KW = 128
SUBS = 8
COLN = 16
GRPS = 2
CORES = 2
RING = SUBS * GRPS
PAD = 24
WIDE = 128
CHUNK = 256
MESH = pl.DeviceIdType.MESH
F32 = jnp.float32
BF16 = jnp.bfloat16
ROWS = ((1,), (0,))
BACK = ((1,), (1,))


def spectral_tables(total):
    phase = np.arange(total)[:, None] * np.arange(KW)[None, :] % total
    angle = 2.0 * math.pi / total * phase
    table = np.concatenate([np.cos(angle), np.sin(angle)], axis=1).astype(np.float32)
    high = table.astype(jnp.bfloat16)
    low = (table - high.astype(np.float32)).astype(jnp.bfloat16)
    return high, low


def spectrum(scales, limits, total, count):
    waves = jnp.arange(count, dtype=jnp.int32)
    wavef = waves.astype(F32)
    decay = jnp.exp(-0.5 * (2.0 * math.pi * wavef[None, :] * scales[:, None] / total) ** 2)
    factor = jnp.where(waves == 0, 1.0, 2.0).astype(F32) / total
    keep = (waves[None, :] < limits[:, None]).astype(F32)
    values = decay * factor[None, :] * keep
    return jnp.concatenate([values, values], axis=1)


class Group:
    def __init__(self, me, count, device):
        self.me, self.count, self.device = me, count, device


class Exchange:
    def __init__(self, group, sems, row, src_of, dst_of):
        self.group, self.sems, self.row = group, sems, row
        self.src_of, self.dst_of = src_of, dst_of

    def copy(self, peer, slot):
        return pltpu.make_async_remote_copy(
            src_ref=self.src_of(peer),
            dst_ref=self.dst_of(slot),
            send_sem=self.sems.at[2 * self.row, peer],
            recv_sem=self.sems.at[2 * self.row + 1, slot],
            device_id=self.group.device(peer),
            device_id_type=MESH,
        )

    def each(self, act):
        group = self.group

        def step(k, carry):
            act(lax.rem(group.me + k, group.count))
            return carry

        lax.fori_loop(1, group.count, step, 0)

    def start(self):
        self.each(lambda peer: self.copy(peer, self.group.me).start())

    def wait_recv(self):
        self.each(lambda peer: self.copy(peer, peer).wait_recv())

    def wait_send(self):
        self.each(lambda peer: self.copy(peer, peer).wait_send())


def greet(*groups):
    barrier = pltpu.get_barrier_semaphore()
    total = 0
    for group in groups:

        def step(k, carry, group=group):
            peer = lax.rem(group.me + k, group.count)
            pl.semaphore_signal(
                barrier, inc=1, device_id=group.device(peer), device_id_type=MESH
            )
            return carry

        lax.fori_loop(1, group.count, step, 0)
        total += group.count - 1
    pl.semaphore_wait(barrier, total)


def lanes(index):
    return pl.ds(pl.multiple_of(index * WIDE, WIDE), WIDE)


def chunk(index, size=CHUNK):
    return pl.ds(pl.multiple_of(index * size, size), size)


def split(x):
    high = x.astype(BF16)
    return high, (x - high.astype(F32)).astype(BF16)


def mm(a, b, dims):
    return lax.dot_general(a, b, (dims, ((), ())), preferred_element_type=F32)


def mm3(a, b, dims):
    return mm(a[0], b[0], dims) + (mm(a[0], b[1], dims) + mm(a[1], b[0], dims))


def pair_sums(buffer, into):
    for t in range(SUBS):
        into[t] = buffer[2 * t] + buffer[2 * t + 1]


def suffix_sums(rows, into):
    total = rows[SUBS - 1]
    into[SUBS - 1] = total
    for t in range(SUBS - 2, -1, -1):
        total = total + rows[t]
        into[t] = total


def prefix_sums(rows, into):
    total = rows[0]
    into[0] = total
    for t in range(1, SUBS):
        total = total + rows[t]
        into[t] = total


def lagged_sums(rows, into):
    total = jnp.zeros_like(rows[0])
    for t in range(SUBS):
        into[t] = total
        total = total + rows[t]


def fold(x):
    return jnp.sum(x.reshape(x.shape[0] // 8, 8, x.shape[1]), axis=0)


class Sums:
    def __init__(self):
        self.held = None

    def add(self, x0, x1, x2, scale=None):
        d0, d1 = x0 - x1, x1 - x2
        terms = (d0 * x0, d0 * d0, d0 * x1 + d1 * x0, d1 * x1, d0 * d1, d1 * d1)
        terms = [fold(x) for x in terms]
        if scale is not None:
            terms = [x * scale for x in terms]
        self.held = terms if self.held is None else [a + b for a, b in zip(self.held, terms)]

    def tile(self):
        rows = [jnp.sum(x, axis=0, keepdims=True) for x in self.held]
        return jnp.concatenate(rows + [jnp.zeros((1, WIDE), F32)] * 2, axis=0)


INPUTS = (
    "b", "obs", "l0", "traj", "w_in", "w_out", "modes", "thi", "tlo", "spec", "pick", "pick_t",
    "var",
)
OUTPUTS = ("mult", "obs_mult", "incr")
NAMES = (
    "shift", "vpair", "vz", "vcore", "hl", "hb", "hr", "nfw", "mret", "sret", "mful", "efw",
    "m2ret", "tfw", "qret", "m2ful", "afw", "ufw", "gat1", "gat2", "red1", "amp0", "lba", "amp1",
    "bak1", "amp2", "bak2", "red2", "clx",
)


def scratch_list(deep, width, hidden, total_cols):
    piece = deep // RING
    field, every = (RING, piece, width), (SUBS, piece, width)
    amps, flat = (COLN, PAD, width), (PAD, total_cols)
    coef, wide = (RING, PAD, 2 * KW), (GRPS, PAD, total_cols)
    back = (COLN, GRPS, PAD, width)
    out = {
        "fin": ((hidden, deep), F32), "fout": ((deep, hidden), F32),
        "wih": ((hidden, deep), BF16), "wil": ((hidden, deep), BF16),
        "woh": ((deep, hidden), BF16), "wol": ((deep, hidden), BF16),
        "slp": ((width, hidden), F32), "hh": ((width, hidden), BF16), "hl_": ((width, hidden), BF16),
        "zh": ((width, deep), BF16), "zl": ((width, deep), BF16), "ot": ((width, deep), F32),
        "vpad": ((COLN, PAD, deep), F32), "voth": ((COLN // CORES, CORES, PAD, deep), F32),
        "vah": ((GRPS, COLN * PAD, deep), BF16), "val": ((GRPS, COLN * PAD, deep), BF16),
        "seen": ((64, deep), F32), "seen2": ((64, deep), F32), "p3t": ((width, deep), F32),
        "ht": ((width, deep), F32), "qt": ((width, deep), F32),
        "cl": ((GRPS, PAD, 2 * KW), F32),
        "r1": (field, F32), "p3": (field, F32), "q": (field, F32),
        "rb1": ((RING, 8, WIDE), F32), "rb2": ((COLN, 8, WIDE), F32),
    }
    for name in ("lup", "np_", "nbuf", "mup", "sb", "mfull", "ep", "ebuf", "m2up", "tp", "tbuf",
                 "qs", "m2full", "ap", "abuf", "up", "ubuf"):
        out[name] = (field, F32)
    for name in ("nt", "mt", "bt", "sbt", "l0t", "r1t", "et", "m2t", "t1t", "qst"):
        out[name] = (every, F32)
    for i in range(3):
        out[f"am{i}"] = (amps, F32)
        out[f"cb{i}"] = (flat, F32)
        out[f"wd{i}"] = (wide, F32)
        out[f"bk{i}"] = (back, F32)
    for i in (1, 2):
        out[f"gb{i}"] = (coef, F32)
    return out


def kernel(names, *refs):
    x = types.SimpleNamespace(**dict(zip(names, refs)))
    s, c, g = lax.axis_index("sub"), lax.axis_index("col"), lax.axis_index("grp")
    core, z = lax.rem(c, CORES), lax.div(c, CORES)
    r = s * GRPS + g
    deep, hidden, width = x.woh.shape[0], x.woh.shape[1], x.slp.shape[0]
    ring = Group(r, RING, lambda p: {"sub": lax.div(p, GRPS), "grp": lax.rem(p, GRPS)})
    subs = Group(s, SUBS, lambda p: {"sub": p})
    cols = Group(c, COLN, lambda p: {"col": p})
    pair = Group(g, GRPS, lambda p: {"grp": p})
    same = Group(z, COLN // CORES, lambda p: {"col": p * CORES + core})
    chip = Group(core, CORES, lambda p: {"col": z * CORES + p})

    def over(name, group, src, dst):
        return Exchange(group, x.sems, NAMES.index(name), src, dst)

    def next_sub(p):
        return lax.rem(lax.div(p, GRPS) + 1, SUBS)

    def forward(name, src, dst):
        return over(name, ring, lambda p: src.at[p], lambda i: dst.at[i])

    def giving(name, src, dst):
        return over(name, ring, lambda p: src.at[lax.div(p, GRPS)], lambda i: dst.at[i])

    def giving_next(name, src, dst):
        return over(name, ring, lambda p: src.at[next_sub(p)], lambda i: dst.at[i])

    def halves(name, src, dst):
        return over(name, subs, lambda p: src.at[p * GRPS + g], lambda i: dst.at[i])

    def amps(name, src, dst):
        return over(name, cols, lambda p: src.at[p], lambda i: dst.at[:, lanes(i)])

    def backs(name, src, dst):
        return over(name, cols, lambda p: src.at[:, :, lanes(p)], lambda i: dst.at[i])

    def gathers(name, buf):
        return over(name, ring, lambda p: buf.at[r], lambda i: buf.at[i])

    row = NAMES.index("shift")
    shift = pltpu.make_async_remote_copy(
        src_ref=x.l0, dst_ref=x.lup, send_sem=x.sems.at[2 * row, 0],
        recv_sem=x.sems.at[2 * row + 1, 0],
        device_id={"sub": lax.rem(s + SUBS - 1, SUBS)}, device_id_type=MESH,
    )
    vpair = over("vpair", pair, lambda p: x.vpad.at[c], lambda i: x.voth.at[z, core])
    vz = over("vz", same, lambda p: x.voth.at[z, core], lambda i: x.voth.at[i, core])
    vcore = over("vcore", chip, lambda p: x.voth.at[:, core], lambda i: x.voth.at[:, i])
    hl = halves("hl", x.l0, x.l0t)
    hb = halves("hb", x.b, x.bt)
    hr = halves("hr", x.r1, x.r1t)
    nfw = forward("nfw", x.np_, x.nbuf)
    mret = giving_next("mret", x.mt, x.mup)
    sret = giving("sret", x.sbt, x.sb)
    mful = giving("mful", x.mt, x.mfull)
    efw = forward("efw", x.ep, x.ebuf)
    m2ret = giving_next("m2ret", x.m2t, x.m2up)
    tfw = forward("tfw", x.tp, x.tbuf)
    qret = giving("qret", x.qst, x.qs)
    m2ful = giving("m2ful", x.m2t, x.m2full)
    afw = forward("afw", x.ap, x.abuf)
    ufw = forward("ufw", x.up, x.ubuf)
    gat1, gat2 = gathers("gat1", x.gb1), gathers("gat2", x.gb2)
    red1 = gathers("red1", x.rb1)
    red2 = over("red2", cols, lambda p: x.rb2.at[c], lambda i: x.rb2.at[i])
    amp0, amp1, amp2 = (amps(f"amp{i}", getattr(x, f"am{i}"), getattr(x, f"cb{i}")) for i in range(3))
    lba, bak1, bak2 = (
        backs(n, getattr(x, f"wd{i}"), getattr(x, f"bk{i}"))
        for i, n in enumerate(("lba", "bak1", "bak2"))
    )
    clx = over("clx", pair, lambda p: x.cl.at[g], lambda i: x.cl.at[i])
    sent = [vpair, vz, vcore, hl, hb, hr, nfw, mret, sret, mful, efw, m2ret, tfw, qret, m2ful,
            afw, ufw, gat1, gat2, red1, red2, amp0, amp1, amp2, lba, bak1, bak2, clx]

    get_in = pltpu.make_async_copy(x.w_in, x.fin, x.local.at[0])
    get_out = pltpu.make_async_copy(x.w_out, x.fout, x.local.at[1])
    get_in.start()
    get_out.start()

    def first_half(columns):
        weights = (x.woh, x.wol) if columns else (x.wih, x.wil)

        def step(j, carry):
            at = (slice(None), chunk(j)) if columns else (chunk(j), slice(None))
            pair_ = (weights[0][at], weights[1][at])
            value = mm3((x.zh[...], x.zl[...]), pair_, ROWS if columns else BACK)
            high, low = split(value * x.slp[:, chunk(j)])
            x.hh[:, chunk(j)] = high
            x.hl_[:, chunk(j)] = low
            return carry

        lax.fori_loop(0, hidden // CHUNK, step, 0)

    def second_half(columns):
        weights = (x.wih, x.wil) if columns else (x.woh, x.wol)

        def part(at):
            where = (slice(None), at) if columns else (at, slice(None))
            pair_ = (weights[0][where], weights[1][where])
            x.ot[:, at] = mm3((x.hh[...], x.hl_[...]), pair_, ROWS if columns else BACK)

        def step(j, carry):
            part(chunk(j))
            return carry

        lax.fori_loop(0, deep // CHUNK, step, 0)
        left = deep % CHUNK
        if left:
            part(pl.ds(deep - left, left))

    def adjoint(zt):
        x.zh[...], x.zl[...] = split(zt)
        first_half(True)
        second_half(True)
        return x.ot[...]

    def tangent(zt):
        x.zh[...], x.zl[...] = split(zt)
        first_half(False)
        second_half(False)
        return x.ot[...]

    def whole(ref):
        return ref[...].reshape(deep, width)

    def put(ref, value_t):
        ref[...] = value_t.T.reshape(ref.shape)

    def amplitudes(ref, into):
        value = mm3((x.vah[g], x.val[g]), split(whole(ref)), ROWS)
        into[...] = value.reshape(into.shape)

    def restored_t(bk):
        total = None
        for h in range(GRPS):
            turned = split(bk[:, h].reshape(COLN * PAD, width).T)
            term = mm3(turned, (x.vah[h], x.val[h]), ROWS)
            total = term if total is None else total + term
        return total

    tables = (x.thi, x.tlo)

    def coefficients(cb):
        return mm3(split(cb[...]), (x.thi[...], x.tlo[...]), ROWS) * x.spec[...]

    def spread_back(values, into):
        value = mm3(split(values), (x.thi[...], x.tlo[...]), BACK)
        into[...] = value.reshape(into.shape)

    def summed(gb):
        parts = []
        for h in range(GRPS):
            total = gb[GRPS * (SUBS - 1) + h]
            for u in range(SUBS - 1):
                total = total + jnp.where(u + 1 <= s, 1.0, 0.0) * gb[GRPS * u + h]
            parts.append(total)
        return jnp.concatenate(parts, axis=0)

    def pick_rows(vt):
        high, low = split(vt)
        return mm(x.pick_t[...], high, ROWS) + mm(x.pick_t[...], low, ROWS)

    def spread_rows(values):
        high, low = split(values)
        return mm(x.pick[...], high, ROWS) + mm(x.pick[...], low, ROWS)

    has_later = jnp.where(s < SUBS - 1, 1.0, 0.0)
    leads = jnp.where(g == 0, 1.0, 0.0)

    owned = x.modes.shape[0] // COLN
    for i in range(COLN):
        x.vpad[i, :owned] = x.modes[i * owned:(i + 1) * owned]
        x.vpad[i, owned:] = jnp.zeros((PAD - owned, deep), F32)
    greet(ring, cols)
    shift.start()
    vpair.start()
    hb.start()
    hl.start()
    x.bt[s] = x.b[r]
    x.l0t[s] = x.l0[r]
    traj_t = x.traj[...].astype(F32).T
    x.zh[...] = traj_t.astype(BF16)
    get_in.wait()

    def open_in(j, carry):
        high, low = split(x.fin[chunk(j), :])
        x.wih[chunk(j), :] = high
        x.wil[chunk(j), :] = low
        inner = mm(x.zh[...], high, BACK) + mm(x.zh[...], low, BACK)
        x.slp[:, chunk(j)] = 1.0 - jnp.tanh(inner) ** 2
        return carry

    lax.fori_loop(0, hidden // CHUNK, open_in, 0)
    get_out.wait()

    def open_out(j, carry):
        high, low = split(x.fout[chunk(j, 64), :])
        x.woh[chunk(j, 64), :] = high
        x.wol[chunk(j, 64), :] = low
        return carry

    lax.fori_loop(0, deep // 64, open_out, 0)
    high, low = split(x.vpad[...].reshape(COLN * PAD, deep))
    x.vah[g] = high
    x.val[g] = low
    shift.wait_recv()
    put(x.np_, adjoint(whole(x.lup).T) * has_later)
    nfw.start()
    x.nbuf[r] = x.np_[r]
    amplitudes(x.l0, x.am0)
    vpair.wait_recv()
    amp0.start()
    vz.start()
    x.cb0[:, lanes(c)] = x.am0[c]
    x.ht[...] = spread_rows(x.obs[...] / x.var[...])
    nfw.wait_recv()
    pair_sums(x.nbuf, x.nt)
    suffix_sums(x.nt, x.mt)
    mret.start()
    x.mup[r] = x.mt[lax.rem(s + 1, SUBS)]
    hb.wait_recv()
    prefix_sums(x.bt, x.sbt)
    sret.start()
    x.sb[r] = x.sbt[s]
    amp0.wait_recv()
    x.cl[g] = coefficients(x.cb0)
    mret.wait_recv()
    amplitudes(x.mup, x.am1)
    amp1.start()
    clx.start()
    x.cb1[:, lanes(c)] = x.am1[c]
    vz.wait_recv()
    vcore.start()
    put(x.ep, adjoint((whole(x.mup) - whole(x.lup)).T) * has_later - leads * x.ht[...])
    amp1.wait_recv()
    x.gb1[r] = coefficients(x.cb1)
    gat1.start()
    efw.start()
    x.ebuf[r] = x.ep[r]
    clx.wait_recv()
    spread_back(x.cl[...].reshape(GRPS * PAD, 2 * KW), x.wd0)
    vcore.wait_recv()
    high, low = split(x.voth[...].reshape(COLN * PAD, deep))
    x.vah[1 - g] = high
    x.val[1 - g] = low
    gat1.wait_recv()
    spread_back(summed(x.gb1), x.wd1)
    bak1.start()
    x.bk1[c] = x.wd1[:, :, lanes(c)]
    efw.wait_recv()
    pair_sums(x.ebuf, x.et)
    suffix_sums(x.et, x.m2t)
    m2ret.start()
    x.m2up[r] = x.m2t[lax.rem(s + 1, SUBS)]
    m2ret.wait_recv()
    amplitudes(x.m2up, x.am2)
    amp2.start()
    lba.start()
    x.cb2[:, lanes(c)] = x.am2[c]
    x.bk0[c] = x.wd0[:, :, lanes(c)]
    sret.wait_recv()
    bak1.wait_recv()
    p3t = whole(x.sb).T - restored_t(x.bk1)
    x.p3t[...] = p3t
    put(x.tp, tangent(p3t))
    tfw.start()
    x.tbuf[r] = x.tp[r]
    amp2.wait_recv()
    x.gb2[r] = coefficients(x.cb2)
    gat2.start()
    put(x.p3, x.p3t[...])
    x.seen[...] = pick_rows(x.p3t[...])
    tfw.wait_recv()
    pair_sums(x.tbuf, x.t1t)
    lagged_sums(x.t1t, x.qst)
    qret.start()
    x.qs[r] = x.qst[s]
    gat2.wait_recv()
    spread_back(summed(x.gb2), x.wd2)
    bak2.start()
    x.bk2[c] = x.wd2[:, :, lanes(c)]
    a2 = adjoint(whole(x.m2up).T) * has_later
    put(x.ap, a2 + leads * spread_rows(x.seen[...] / x.var[...]))
    afw.start()
    x.abuf[r] = x.ap[r]
    lba.wait_recv()
    x.r1[...] = x.b[...] - restored_t(x.bk0).T.reshape(x.r1.shape)
    hr.start()
    x.r1t[s] = x.r1[r]
    qret.wait_recv()
    bak2.wait_recv()
    qt = whole(x.qs).T - restored_t(x.bk2)
    x.qt[...] = qt
    put(x.up, tangent(qt))
    ufw.start()
    mful.start()
    m2ful.start()
    x.ubuf[r] = x.up[r]
    x.mfull[r] = x.mt[s]
    x.m2full[r] = x.m2t[s]
    put(x.q, x.qt[...])
    x.seen2[...] = pick_rows(x.qt[...])
    sums = Sums()
    for i in range(deep // WIDE):
        at = slice(i * WIDE, (i + 1) * WIDE)
        sums.add(x.obs[:, at], -x.seen[:, at], -x.seen2[:, at], leads)
    hl.wait_recv()
    afw.wait_recv()
    blank = jnp.zeros_like(x.mt[0])
    for t in range(SUBS):
        here = x.mt[t] - x.l0t[t]
        later = x.mt[t + 1] - x.l0t[t + 1] if t < SUBS - 1 else blank
        sums.add(here - later, x.et[t], x.abuf[2 * t] + x.abuf[2 * t + 1])
    hr.wait_recv()
    ufw.wait_recv()
    for t in range(SUBS):
        x1 = x.t1t[t - 1] if t else blank
        x2 = x.ubuf[2 * t - 2] + x.ubuf[2 * t - 1] if t else blank
        sums.add(x.r1t[t], x1, x2)
    x.rb1[r] = sums.tile()
    red1.start()
    red1.wait_recv()
    total = x.rb1[0]
    for i in range(1, RING):
        total = total + x.rb1[i]
    x.rb2[c] = total
    red2.start()
    mful.wait_recv()
    m2ful.wait_recv()
    red2.wait_recv()
    total = x.rb2[0]
    for i in range(1, COLN):
        total = total + x.rb2[i]
    gram = jnp.sum(total, axis=1, keepdims=True)
    gram = [gram[i:i + 1] for i in range(6)]
    a = gram[0] / gram[1]
    b = 1.0 - a
    upper = b * b * gram[0] + a * b * gram[2] + a * a * gram[3]
    lower = b * b * gram[1] + 2.0 * a * b * gram[4] + a * a * gram[5]
    a_next = upper / lower
    start = whole(x.l0)
    move = whole(x.mfull) - start
    mult = start + a * move + a_next * (b * move + a * whole(x.m2full))
    x.mult[...] = mult.reshape(x.mult.shape)
    p3 = whole(x.p3)
    x.incr[...] = (a * p3 + a_next * (b * p3 + a * whole(x.q))).reshape(x.incr.shape)
    obs = x.obs[...]
    x.obs_mult[...] = (a * obs + a_next * (b * obs - a * x.seen[...])) / x.var[...]
    for one in sent:
        one.wait_send()
    shift.wait_send()


def on_device(
    first_rhs,
    innovations,
    start_mult,
    trajectory,
    weight_in,
    weight_out,
    vertical_modes,
    length_scale,
    band_limit,
    obs_col,
    obs_count,
    obs_var,
):
    deep, width = first_rhs.shape[1:]
    slots = innovations.shape[1]
    hidden = weight_in.shape[0]
    c, g = lax.axis_index("col"), lax.axis_index("grp")
    total_cols = width * COLN
    half = vertical_modes.shape[0]
    owned = half // COLN
    field = (RING, deep // RING, width)
    thi, tlo = (jnp.asarray(x) for x in spectral_tables(total_cols))

    first_mode = g * half + c * owned
    scales = lax.dynamic_slice_in_dim(length_scale, first_mode, owned, 0)
    limits = lax.dynamic_slice_in_dim(band_limit, first_mode, owned, 0)
    spec = jnp.pad(spectrum(scales, limits, total_cols, KW), ((0, PAD - owned), (0, 0)))
    local_cols = obs_col[0] - c * width
    live = jnp.arange(slots, dtype=jnp.int32) < obs_count[0, 0]
    chosen = jnp.where(live, local_cols, -1)
    columns = jnp.arange(width, dtype=jnp.int32)
    pick = (columns[:, None] == chosen[None, :]).astype(BF16)
    pick_t = (chosen[:, None] == columns[None, :]).astype(BF16)

    vmem = pl.BlockSpec(memory_space=pltpu.VMEM)
    away = pl.BlockSpec(memory_space=pl.ANY)
    args = dict(
        b=first_rhs.reshape(field), obs=innovations[0], l0=start_mult.reshape(field),
        traj=trajectory[0], w_in=weight_in, w_out=weight_out, modes=vertical_modes,
        thi=thi, tlo=tlo, spec=spec, pick=pick, pick_t=pick_t, var=obs_var[0][:, None],
    )
    scratch = scratch_list(deep, width, hidden, total_cols)
    names = INPUTS + OUTPUTS + tuple(scratch) + ("local", "sems")
    shapes = (field, (slots, deep), field)
    mult, obs_mult, incr = pl.pallas_call(
        lambda *refs: kernel(names, *refs),
        name="saddle",
        out_shape=[jax.ShapeDtypeStruct(shape, F32) for shape in shapes],
        in_specs=[away if n in ("w_in", "w_out") else vmem for n in INPUTS],
        out_specs=[vmem] * len(shapes),
        scratch_shapes=[pltpu.VMEM(*scratch[n]) for n in scratch]
        + [pltpu.SemaphoreType.DMA((2,)), pltpu.SemaphoreType.DMA((2 * len(NAMES), 16))],
        compiler_params=pltpu.CompilerParams(collective_id=0, has_side_effects=True),
    )(*(args[n] for n in INPUTS))
    return (
        mult.reshape(1, deep, width), obs_mult[None], incr.reshape(1, deep, width)
    )


def solution(mesh):
    in_specs = (
        P("sub", None, "col"),
        P("sub", "col", None),
        P("sub", None, "col"),
        P("sub", None, "col"),
        P("grp", None),
        P(None, "grp"),
        P("grp", None),
        P(),
        P(),
        P("sub", "col"),
        P("sub", "col"),
        P("sub", "col"),
    )
    out_specs = (P("sub", None, "col"), P("sub", "col", None), P("sub", None, "col"))
    return jax.shard_map(
        on_device, mesh=mesh, in_specs=in_specs, out_specs=out_specs, check_vma=False
    )
```

time: 561 us -> 158 us (0.28); the launches traced: 550 us -> 158 us
  blocking collectives: 151 us -> 0 us
  Pallas kernels: 0 us -> 145 us
  waiting for transfers between devices: 143 us -> 0 us
  matrix products: 104 us -> 0 us
  starting transfers between devices: 66.7 us -> 0 us
  other arithmetic: 34.4 us -> 3.32 us
  between operations: 26.1 us -> 1.3 us
  local copies, waits for them, and re-layouts: 24 us -> 7.91 us
    pallas_call x0 -> x1, Pallas kernels: none -> 145 us  [on_device(): pl.pallas_call(lambda *refs: kernel(names, *refs), name='saddle', out_sha...]
    dot_general x27 -> x0, matrix products: 104 us -> none  [the longest x9 50.9 us: product_first(): lax.dot_general(left, right, (((0,), (0,)), ((), ())), precision=HIGH, pr...]
    psum x8 -> x0, blocking collectives: 87.2 us -> none  [over_axes(): return functools.reduce(lax.psum, axes, array)]
    all_gather x4 -> x0, waiting for transfers between devices: 71.8 us -> none  [running(): every = lax.all_gather(field[None], SUB, axis=0, tiled=True)]
    all_to_all x4 -> x0, blocking collectives: 64.2 us -> none  [the longest x2 29.8 us: sent_to_all(): lax.all_to_all(jnp.broadcast_to(array[None], (length, *array.shape)), axi...]
    all_to_all x10 -> x0, starting transfers between devices: 54.6 us -> none  [the longest x6 25.1 us: sent_to_all(): lax.all_to_all(jnp.broadcast_to(array[None], (length, *array.shape)), axi...]
    all_to_all x10 -> x0, waiting for transfers between devices: 46.9 us -> none  [the longest x6 25.6 us: sent_to_all(): lax.all_to_all(jnp.broadcast_to(array[None], (length, *array.shape)), axi...]
    ppermute x5 -> x0, waiting for transfers between devices: 24.5 us -> none  [passed_along(): return lax.ppermute(block, axis, route)]
  transfers between devices with their start and end apart: 19 -> 0, of which waited for: 15 -> 0; matrix products, arithmetic and copies ran while one was open for 17% -> 0% of each run, Pallas kernels for 0% -> 0%
where the time goes in v1:
time: 158 us
  Pallas kernels  145 us (92%)
  local copies, waits for them, and re-layouts  7.91 us (5%)
  other arithmetic  3.32 us (2%)
    pallas_call x1, Pallas kernels, on_device(): pl.pallas_call(lambda *refs: kernel(names, *refs), name='saddle', out_sha...  145 us
    unnamed x3, local copies, waits for them, and re-layouts  5.03 us

profile of v1, /device:TPU:1, one launch (start us, length us, event | category | flops | bytes accessed | tf_op | source)
XLA Modules:
  0.0 157.6 jit_solution(12254629891327775851)
XLA Ops:
  1.3 0.8 dynamic_slice.7
  2.0 0.8 dynamic_slice.6
  2.8 0.7 compare_select_fusion
  3.5 0.7 fusion.3
  4.1 0.1 multiply_select_fusion
  4.2 0.6 select_maximum_fusion.refs_9_
  4.8 0.7 fusion.1.refs_11_
  5.5 0.6 fusion.refs_10_
  6.1 1.4 copy.17.refs_12_
  7.5 145.0 %saddle.1 = (f32[16,40,128]{2,1,0:T(8,128)}, f32[64,640]{1,0:T(8,128)}, f32[16,40,128]{2,1,0:T(8,128)}) custom-call(f32[16,40,128]{2,1,0:T(8,128)} %bitcast.17, f32[64,640]{1,0:T(8,128)} %bitcast.19, f32[16,40,128]{2,1,0:T(8,128)} %bitcast.18, bf16[640,128]{1,0:T(8,128)(2,1)} %bitcast.20, f32[2048,640]{1,0:T(8,128)} %refs_4_.1, f32[640,2048]{1,0:T(8,128)} %refs_5_.1, ...), custom_call_target="tpu_custom_call" | custom-call | tf_op jit(solution)/shard_map/saddle/pallas_call | solution.py:619
  152.5 1.7 %copy.22 = f32[1,640,128]{2,1,0:T(8,128)} copy(f32[1,640,128]{2,1,0:T(8,128)} %bitcast.16) | data formatting | bytes 655360
  154.2 1.6 %copy.23 = f32[1,64,640]{2,1,0:T(8,128)} copy(f32[1,64,640]{2,1,0:T(8,128)} %bitcast.21) | data formatting | bytes 327680
  155.8 1.7 %copy.24 = f32[1,640,128]{2,1,0:T(8,128)} copy(f32[1,640,128]{2,1,0:T(8,128)} %bitcast.15) | data formatting | bytes 655360
  (1 shorter events, 0.0 us)

commit v2 on v1

--- a/solution.py
+++ b/solution.py
@@ -25,23 +25,14 @@
 BACK = ((1,), (1,))
 
 
-def spectral_tables(total):
-    phase = np.arange(total)[:, None] * np.arange(KW)[None, :] % total
-    angle = 2.0 * math.pi / total * phase
-    table = np.concatenate([np.cos(angle), np.sin(angle)], axis=1).astype(np.float32)
-    high = table.astype(jnp.bfloat16)
-    low = (table - high.astype(np.float32)).astype(jnp.bfloat16)
-    return high, low
-
-
-def spectrum(scales, limits, total, count):
-    waves = jnp.arange(count, dtype=jnp.int32)
-    wavef = waves.astype(F32)
-    decay = jnp.exp(-0.5 * (2.0 * math.pi * wavef[None, :] * scales[:, None] / total) ** 2)
-    factor = jnp.where(waves == 0, 1.0, 2.0).astype(F32) / total
-    keep = (waves[None, :] < limits[:, None]).astype(F32)
-    values = decay * factor[None, :] * keep
-    return jnp.concatenate([values, values], axis=1)
+def base_tables(total):
+    waves = np.arange(KW)[None, :]
+    inner, outer = np.arange(WIDE)[:, None], np.arange(0, total, WIDE)[:, None]
+    parts = []
+    for columns in (inner, outer):
+        angle = 2.0 * math.pi / total * (columns * waves % total)
+        parts += [np.cos(angle), np.sin(angle)]
+    return np.concatenate(parts, axis=0).astype(np.float32)
 
 
 class Group:
@@ -83,9 +74,8 @@
         self.each(lambda peer: self.copy(peer, peer).wait_send())
 
 
-def greet(*groups):
+def meet(*groups):
     barrier = pltpu.get_barrier_semaphore()
-    total = 0
     for group in groups:
 
         def step(k, carry, group=group):
@@ -96,8 +86,10 @@
             return carry
 
         lax.fori_loop(1, group.count, step, 0)
-        total += group.count - 1
-    pl.semaphore_wait(barrier, total)
+
+
+def met(*groups):
+    pl.semaphore_wait(pltpu.get_barrier_semaphore(), sum(g.count - 1 for g in groups))
 
 
 def lanes(index):
@@ -119,6 +111,16 @@
 
 def mm3(a, b, dims):
     return mm(a[0], b[0], dims) + (mm(a[0], b[1], dims) + mm(a[1], b[0], dims))
+
+
+def stack(x):
+    return jnp.concatenate(split(x), axis=0)
+
+
+def mm3s(both, b, dims):
+    rows = both.shape[0] // 2
+    value = mm(both, b[0], dims)
+    return value[:rows] + value[rows:] + mm(both[:rows], b[1], dims)
 
 
 def pair_sums(buffer, into):
@@ -171,10 +173,10 @@
 
 
 INPUTS = (
-    "b", "obs", "l0", "traj", "w_in", "w_out", "modes", "thi", "tlo", "spec", "pick", "pick_t",
-    "var",
+    "b", "obs", "l0", "traj", "w_in", "w_out", "modes", "base", "scale", "limit", "ocol", "count",
+    "vrow",
 )
-OUTPUTS = ("mult", "obs_mult", "incr")
+OUTPUTS = ("mult", "obs_a", "obs_b", "incr_a", "incr_b")
 NAMES = (
     "shift", "vpair", "vz", "vcore", "hl", "hb", "hr", "nfw", "mret", "sret", "mful", "efw",
     "m2ret", "tfw", "qret", "m2ful", "afw", "ufw", "gat1", "gat2", "red1", "amp0", "lba", "amp1",
@@ -192,13 +194,16 @@
         "fin": ((hidden, deep), F32), "fout": ((deep, hidden), F32),
         "wih": ((hidden, deep), BF16), "wil": ((hidden, deep), BF16),
         "woh": ((deep, hidden), BF16), "wol": ((deep, hidden), BF16),
-        "slp": ((width, hidden), F32), "hh": ((width, hidden), BF16), "hl_": ((width, hidden), BF16),
-        "zh": ((width, deep), BF16), "zl": ((width, deep), BF16), "ot": ((width, deep), F32),
+        "slp": ((width, hidden), F32), "hh": ((2 * width, hidden), BF16),
+        "zz": ((2 * width, deep), BF16), "ot": ((width, deep), F32),
         "vpad": ((COLN, PAD, deep), F32), "voth": ((COLN // CORES, CORES, PAD, deep), F32),
         "vah": ((GRPS, COLN * PAD, deep), BF16), "val": ((GRPS, COLN * PAD, deep), BF16),
         "seen": ((64, deep), F32), "seen2": ((64, deep), F32), "p3t": ((width, deep), F32),
         "ht": ((width, deep), F32), "qt": ((width, deep), F32),
         "cl": ((GRPS, PAD, 2 * KW), F32),
+        "thi": ((total_cols, 2 * KW), BF16), "tlo": ((total_cols, 2 * KW), BF16),
+        "spec": ((PAD, 2 * KW), F32), "var": ((64, 1), F32), "fmod": ((deep // GRPS, deep), F32),
+        "pick": ((width, 64), BF16), "pick_t": ((64, width), BF16),
         "r1": (field, F32), "p3": (field, F32), "q": (field, F32),
         "rb1": ((RING, 8, WIDE), F32), "rb2": ((COLN, 8, WIDE), F32),
     }
@@ -295,7 +300,9 @@
     get_in = pltpu.make_async_copy(x.w_in, x.fin, x.local.at[0])
     get_out = pltpu.make_async_copy(x.w_out, x.fout, x.local.at[1])
     get_in.start()
+    get_modes = pltpu.make_async_copy(x.modes, x.fmod, x.local.at[2])
     get_out.start()
+    get_modes.start()
 
     def first_half(columns):
         weights = (x.woh, x.wol) if columns else (x.wih, x.wil)
@@ -303,10 +310,8 @@
         def step(j, carry):
             at = (slice(None), chunk(j)) if columns else (chunk(j), slice(None))
             pair_ = (weights[0][at], weights[1][at])
-            value = mm3((x.zh[...], x.zl[...]), pair_, ROWS if columns else BACK)
-            high, low = split(value * x.slp[:, chunk(j)])
-            x.hh[:, chunk(j)] = high
-            x.hl_[:, chunk(j)] = low
+            value = mm3s(x.zz[...], pair_, ROWS if columns else BACK)
+            x.hh[:, chunk(j)] = stack(value * x.slp[:, chunk(j)])
             return carry
 
         lax.fori_loop(0, hidden // CHUNK, step, 0)
@@ -317,7 +322,7 @@
         def part(at):
             where = (slice(None), at) if columns else (at, slice(None))
             pair_ = (weights[0][where], weights[1][where])
-            x.ot[:, at] = mm3((x.hh[...], x.hl_[...]), pair_, ROWS if columns else BACK)
+            x.ot[:, at] = mm3s(x.hh[...], pair_, ROWS if columns else BACK)
 
         def step(j, carry):
             part(chunk(j))
@@ -329,14 +334,15 @@
             part(pl.ds(deep - left, left))
 
     def adjoint(zt):
-        x.zh[...], x.zl[...] = split(zt)
+        x.zz[...] = stack(zt)
         first_half(True)
         second_half(True)
         return x.ot[...]
 
-    def tangent(zt):
-        x.zh[...], x.zl[...] = split(zt)
+    def tangent(zt, between=lambda: None):
+        x.zz[...] = stack(zt)
         first_half(False)
+        between()
         second_half(False)
         return x.ot[...]
 
@@ -347,24 +353,24 @@
         ref[...] = value_t.T.reshape(ref.shape)
 
     def amplitudes(ref, into):
-        value = mm3((x.vah[g], x.val[g]), split(whole(ref)), ROWS)
+        high, low = split(whole(ref))
+        value = mm(x.vah[g], jnp.concatenate([high, low], axis=1), ROWS)
+        value = value[:, :width] + value[:, width:] + mm(x.val[g], high, ROWS)
         into[...] = value.reshape(into.shape)
 
     def restored_t(bk):
         total = None
         for h in range(GRPS):
-            turned = split(bk[:, h].reshape(COLN * PAD, width).T)
-            term = mm3(turned, (x.vah[h], x.val[h]), ROWS)
+            turned = stack(bk[:, h].reshape(COLN * PAD, width).T)
+            term = mm3s(turned, (x.vah[h], x.val[h]), ROWS)
             total = term if total is None else total + term
         return total
 
-    tables = (x.thi, x.tlo)
-
     def coefficients(cb):
         return mm3(split(cb[...]), (x.thi[...], x.tlo[...]), ROWS) * x.spec[...]
 
     def spread_back(values, into):
-        value = mm3(split(values), (x.thi[...], x.tlo[...]), BACK)
+        value = mm3s(stack(values), (x.thi[...], x.tlo[...]), BACK)
         into[...] = value.reshape(into.shape)
 
     def summed(gb):
@@ -388,25 +394,21 @@
     leads = jnp.where(g == 0, 1.0, 0.0)
 
     owned = x.modes.shape[0] // COLN
-    for i in range(COLN):
-        x.vpad[i, :owned] = x.modes[i * owned:(i + 1) * owned]
-        x.vpad[i, owned:] = jnp.zeros((PAD - owned, deep), F32)
-    greet(ring, cols)
+    meet(ring, cols)
+    traj_t = x.traj[...].astype(F32).T
+    x.zz[:width] = traj_t.astype(BF16)
+    met(ring, cols)
     shift.start()
-    vpair.start()
     hb.start()
-    hl.start()
     x.bt[s] = x.b[r]
     x.l0t[s] = x.l0[r]
-    traj_t = x.traj[...].astype(F32).T
-    x.zh[...] = traj_t.astype(BF16)
     get_in.wait()
 
     def open_in(j, carry):
         high, low = split(x.fin[chunk(j), :])
         x.wih[chunk(j), :] = high
         x.wil[chunk(j), :] = low
-        inner = mm(x.zh[...], high, BACK) + mm(x.zh[...], low, BACK)
+        inner = mm(x.zz[:width], high, BACK) + mm(x.zz[:width], low, BACK)
         x.slp[:, chunk(j)] = 1.0 - jnp.tanh(inner) ** 2
         return carry
 
@@ -420,18 +422,65 @@
         return carry
 
     lax.fori_loop(0, deep // 64, open_out, 0)
-    high, low = split(x.vpad[...].reshape(COLN * PAD, deep))
-    x.vah[g] = high
-    x.val[g] = low
     shift.wait_recv()
     put(x.np_, adjoint(whole(x.lup).T) * has_later)
     nfw.start()
     x.nbuf[r] = x.np_[r]
+    get_modes.wait()
+    for i in range(COLN):
+        x.vpad[i, :owned] = x.fmod[i * owned:(i + 1) * owned]
+        x.vpad[i, owned:] = jnp.zeros((PAD - owned, deep), F32)
+    vpair.start()
+    high, low = split(x.vpad[...].reshape(COLN * PAD, deep))
+    x.vah[g] = high
+    x.val[g] = low
     amplitudes(x.l0, x.am0)
+    amp0.start()
+    x.cb0[:, lanes(c)] = x.am0[c]
+
+    def iota(shape, dim):
+        return lax.broadcasted_iota(jnp.int32, shape, dim)
+
+    total_cols = width * COLN
+    first_mode = g * (owned * COLN) + c * owned
+    scales = limits = jnp.zeros((PAD, WIDE), F32)
+    for q in range(deep // WIDE):
+        own = iota((PAD, WIDE), 1) + q * WIDE == iota((PAD, WIDE), 0) + first_mode
+        scales = scales + jnp.where(own, x.scale[q:q + 1, :], 0.0)
+        limits = limits + jnp.where(own, x.limit[q:q + 1, :].astype(F32), 0.0)
+    scales = jnp.sum(scales, axis=1, keepdims=True)
+    limits = jnp.sum(limits, axis=1, keepdims=True)
+    wave = iota((PAD, KW), 1).astype(F32)
+    decay = jnp.exp(-0.5 * (2.0 * math.pi * wave * scales / total_cols) ** 2)
+    factor = jnp.where(iota((PAD, KW), 1) == 0, 1.0, 2.0) / total_cols
+    values = decay * factor * jnp.where(wave < limits, 1.0, 0.0)
+    x.spec[:, :KW] = values
+    x.spec[:, KW:] = values
+    slots = x.obs.shape[0]
+    chosen = jnp.where(iota((1, slots), 1) < x.count[...], x.ocol[...] - c * width, -1)
+    chosen = chosen.astype(F32)
+    eye = iota((slots, slots), 0) == iota((slots, slots), 1)
+    down = jnp.sum(jnp.where(eye, chosen, 0.0), axis=1, keepdims=True)
+    x.var[...] = jnp.sum(jnp.where(eye, x.vrow[...], 0.0), axis=1, keepdims=True)
+    near = iota((width, slots), 0).astype(F32) == chosen
+    x.pick[...] = jnp.where(near, 1.0, 0.0).astype(BF16)
+    near = iota((slots, width), 1).astype(F32) == down
+    x.pick_t[...] = jnp.where(near, 1.0, 0.0).astype(BF16)
+
+    def open_table(p, carry):
+        cos_in, sin_in = x.base[:WIDE], x.base[WIDE:2 * WIDE]
+        cos_at = x.base[pl.ds(2 * WIDE + p, 1)]
+        sin_at = x.base[pl.ds(2 * WIDE + COLN + p, 1)]
+        rows = chunk(p, WIDE)
+        high, low = split(cos_at * cos_in - sin_at * sin_in)
+        x.thi[rows, :KW], x.tlo[rows, :KW] = high, low
+        high, low = split(sin_at * cos_in + cos_at * sin_in)
+        x.thi[rows, KW:], x.tlo[rows, KW:] = high, low
+        return carry
+
+    lax.fori_loop(0, COLN, open_table, 0)
     vpair.wait_recv()
-    amp0.start()
     vz.start()
-    x.cb0[:, lanes(c)] = x.am0[c]
     x.ht[...] = spread_rows(x.obs[...] / x.var[...])
     nfw.wait_recv()
     pair_sums(x.nbuf, x.nt)
@@ -442,6 +491,8 @@
     prefix_sums(x.bt, x.sbt)
     sret.start()
     x.sb[r] = x.sbt[s]
+    mful.start()
+    x.mfull[r] = x.mt[s]
     amp0.wait_recv()
     x.cl[g] = coefficients(x.cb0)
     mret.wait_recv()
@@ -471,6 +522,8 @@
     pair_sums(x.ebuf, x.et)
     suffix_sums(x.et, x.m2t)
     m2ret.start()
+    m2ful.start()
+    x.m2full[r] = x.m2t[s]
     x.m2up[r] = x.m2t[lax.rem(s + 1, SUBS)]
     m2ret.wait_recv()
     amplitudes(x.m2up, x.am2)
@@ -482,12 +535,19 @@
     bak1.wait_recv()
     p3t = whole(x.sb).T - restored_t(x.bk1)
     x.p3t[...] = p3t
-    put(x.tp, tangent(p3t))
+
+    def between():
+        amp2.wait_recv()
+        x.gb2[r] = coefficients(x.cb2)
+        gat2.start()
+
+    put(x.tp, tangent(p3t, between))
     tfw.start()
     x.tbuf[r] = x.tp[r]
-    amp2.wait_recv()
-    x.gb2[r] = coefficients(x.cb2)
-    gat2.start()
+    gat2.wait_recv()
+    spread_back(summed(x.gb2), x.wd2)
+    bak2.start()
+    x.bk2[c] = x.wd2[:, :, lanes(c)]
     put(x.p3, x.p3t[...])
     x.seen[...] = pick_rows(x.p3t[...])
     tfw.wait_recv()
@@ -495,10 +555,6 @@
     lagged_sums(x.t1t, x.qst)
     qret.start()
     x.qs[r] = x.qst[s]
-    gat2.wait_recv()
-    spread_back(summed(x.gb2), x.wd2)
-    bak2.start()
-    x.bk2[c] = x.wd2[:, :, lanes(c)]
     a2 = adjoint(whole(x.m2up).T) * has_later
     put(x.ap, a2 + leads * spread_rows(x.seen[...] / x.var[...]))
     afw.start()
@@ -506,6 +562,7 @@
     lba.wait_recv()
     x.r1[...] = x.b[...] - restored_t(x.bk0).T.reshape(x.r1.shape)
     hr.start()
+    hl.start()
     x.r1t[s] = x.r1[r]
     qret.wait_recv()
     bak2.wait_recv()
@@ -513,11 +570,7 @@
     x.qt[...] = qt
     put(x.up, tangent(qt))
     ufw.start()
-    mful.start()
-    m2ful.start()
     x.ubuf[r] = x.up[r]
-    x.mfull[r] = x.mt[s]
-    x.m2full[r] = x.m2t[s]
     put(x.q, x.qt[...])
     x.seen2[...] = pick_rows(x.qt[...])
     sums = Sums()
@@ -558,14 +611,13 @@
     upper = b * b * gram[0] + a * b * gram[2] + a * a * gram[3]
     lower = b * b * gram[1] + 2.0 * a * b * gram[4] + a * a * gram[5]
     a_next = upper / lower
-    start = whole(x.l0)
-    move = whole(x.mfull) - start
-    mult = start + a * move + a_next * (b * move + a * whole(x.m2full))
-    x.mult[...] = mult.reshape(x.mult.shape)
-    p3 = whole(x.p3)
-    x.incr[...] = (a * p3 + a_next * (b * p3 + a * whole(x.q))).reshape(x.incr.shape)
-    obs = x.obs[...]
-    x.obs_mult[...] = (a * obs + a_next * (b * obs - a * x.seen[...])) / x.var[...]
+    one, two = a + a_next * b, a_next * a
+    move = whole(x.mfull) - whole(x.l0)
+    x.mult[...] = (one * move + two * whole(x.m2full)).reshape(x.mult.shape)
+    x.incr_a[...] = (one * whole(x.p3)).reshape(x.incr_a.shape)
+    x.incr_b[...] = (two * whole(x.q)).reshape(x.incr_b.shape)
+    x.obs_a[...] = one * (x.obs[...] / x.var[...])
+    x.obs_b[...] = two * (x.seen[...] / x.var[...])
     for one in sent:
         one.wait_send()
     shift.wait_send()
@@ -588,47 +640,33 @@
     deep, width = first_rhs.shape[1:]
     slots = innovations.shape[1]
     hidden = weight_in.shape[0]
-    c, g = lax.axis_index("col"), lax.axis_index("grp")
     total_cols = width * COLN
-    half = vertical_modes.shape[0]
-    owned = half // COLN
     field = (RING, deep // RING, width)
-    thi, tlo = (jnp.asarray(x) for x in spectral_tables(total_cols))
-
-    first_mode = g * half + c * owned
-    scales = lax.dynamic_slice_in_dim(length_scale, first_mode, owned, 0)
-    limits = lax.dynamic_slice_in_dim(band_limit, first_mode, owned, 0)
-    spec = jnp.pad(spectrum(scales, limits, total_cols, KW), ((0, PAD - owned), (0, 0)))
-    local_cols = obs_col[0] - c * width
-    live = jnp.arange(slots, dtype=jnp.int32) < obs_count[0, 0]
-    chosen = jnp.where(live, local_cols, -1)
-    columns = jnp.arange(width, dtype=jnp.int32)
-    pick = (columns[:, None] == chosen[None, :]).astype(BF16)
-    pick_t = (chosen[:, None] == columns[None, :]).astype(BF16)
 
     vmem = pl.BlockSpec(memory_space=pltpu.VMEM)
     away = pl.BlockSpec(memory_space=pl.ANY)
     args = dict(
         b=first_rhs.reshape(field), obs=innovations[0], l0=start_mult.reshape(field),
         traj=trajectory[0], w_in=weight_in, w_out=weight_out, modes=vertical_modes,
-        thi=thi, tlo=tlo, spec=spec, pick=pick, pick_t=pick_t, var=obs_var[0][:, None],
+        base=jnp.asarray(base_tables(total_cols)), scale=length_scale.reshape(-1, WIDE),
+        limit=band_limit.reshape(-1, WIDE), ocol=obs_col, count=obs_count, vrow=obs_var,
     )
     scratch = scratch_list(deep, width, hidden, total_cols)
     names = INPUTS + OUTPUTS + tuple(scratch) + ("local", "sems")
-    shapes = (field, (slots, deep), field)
-    mult, obs_mult, incr = pl.pallas_call(
+    shapes = (field, (slots, deep), (slots, deep), field, field)
+    move, obs_a, obs_b, incr_a, incr_b = pl.pallas_call(
         lambda *refs: kernel(names, *refs),
         name="saddle",
         out_shape=[jax.ShapeDtypeStruct(shape, F32) for shape in shapes],
-        in_specs=[away if n in ("w_in", "w_out") else vmem for n in INPUTS],
+        in_specs=[away if n in ("w_in", "w_out", "modes") else vmem for n in INPUTS],
         out_specs=[vmem] * len(shapes),
         scratch_shapes=[pltpu.VMEM(*scratch[n]) for n in scratch]
-        + [pltpu.SemaphoreType.DMA((2,)), pltpu.SemaphoreType.DMA((2 * len(NAMES), 16))],
+        + [pltpu.SemaphoreType.DMA((3,)), pltpu.SemaphoreType.DMA((2 * len(NAMES), 16))],
         compiler_params=pltpu.CompilerParams(collective_id=0, has_side_effects=True),
     )(*(args[n] for n in INPUTS))
-    return (
-        mult.reshape(1, deep, width), obs_mult[None], incr.reshape(1, deep, width)
-    )
+    mult = start_mult + move.reshape(1, deep, width)
+    incr = incr_a + incr_b
+    return mult, (obs_a - obs_b)[None], incr.reshape(1, deep, width)
 
 
 def solution(mesh):

time: 158 us -> 144 us (0.911)
  Pallas kernels: 145 us -> 137 us
  local copies, waits for them, and re-layouts: 7.91 us -> 0.01 us
  other arithmetic: 3.32 us -> 5.24 us
    pallas_call x1, Pallas kernels: 145 us -> 137 us  [on_device(): pl.pallas_call(lambda *refs: kernel(names, *refs), name='saddle', out_sha...]
    unnamed x3 -> x2, local copies, waits for them, and re-layouts: 5.03 us -> 0.01 us
    add x0 -> x2, other arithmetic: none -> 3.56 us  [the longest x1 1.83 us: on_device(): incr = incr_a + incr_b]
    broadcast_in_dim x0 -> x1, other arithmetic: none -> 1.68 us  [on_device(): return (mult, (obs_a - obs_b)[None], incr.reshape(1, deep, width))]
where the time goes in v2:
time: 144 us
  Pallas kernels  137 us (95%)
  other arithmetic  5.24 us (4%)
    pallas_call x1, Pallas kernels, on_device(): pl.pallas_call(lambda *refs: kernel(names, *refs), name='saddle', out_sha...  137 us

profile of v2, /device:TPU:1, one launch (start us, length us, event | category | flops | bytes accessed | tf_op | source)
XLA Modules:
  0.0 143.8 jit_solution(13052753521671256166)
XLA Ops:
  1.3 0.0 copy-start
  1.3 137.2 %saddle.1 = (f32[16,40,128]{2,1,0:T(8,128)}, f32[64,640]{1,0:T(8,128)}, f32[64,640]{1,0:T(8,128)}, f32[16,40,128]{2,1,0:T(8,128)}, f32[16,40,128]{2,1,0:T(8,128)}) custom-call(f32[16,40,128]{2,1,0:T(8,128)} %bitcast.13, f32[64,640]{1,0:T(8,128)} %bitcast.16, f32[16,40,128]{2,1,0:T(8,128)} %bitcast.12, bf16[640,128]{1,0:T(8,128)(2,1)} %bitcast.17, ...), custom_call_target="tpu_custom_call" | custom-call | tf_op jit(solution)/shard_map/saddle/pallas_call | solution.py:657
  138.5 0.0 copy-done
  138.5 1.7 %bitcast_add_fusion = f32[1,640,128]{2,1,0:T(8,128)} fusion(f32[1,640,128]{2,1,0:T(8,128)S(1)} %copy-done, f32[1,640,128]{2,1,0:T(8,128)} %bitcast.15), kind=kLoop, calls=%fused_computation | loop fusion | flops 81920 | bytes 983040 | tf_op jit(solution)/shard_map/add | solution.py:667
  140.3 1.7 %subtract_bitcast_fusion = f32[1,64,640]{2,1,0:T(8,128)} fusion(f32[64,640]{1,0:T(8,128)} %get-tuple-element.9, f32[64,640]{1,0:T(8,128)} %get-tuple-element.10), kind=kLoop, calls=%fused_computation.1 | loop fusion | flops 40960 | bytes 491520 | tf_op jit(solution)/shard_map/broadcast_in_dim | solution.py:669
  141.9 1.8 %add.7 = f32[16,40,128]{2,1,0:T(8,128)} add(f32[16,40,128]{2,1,0:T(8,128)} %get-tuple-element.11, f32[16,40,128]{2,1,0:T(8,128)} %get-tuple-element.12) | non-fusion elementwise | flops 81920 | bytes 983040 | tf_op jit(solution)/shard_map/add | solution.py:668
Async XLA Ops:
  1.3 137.2 %copy-start = (f32[1,640,128]{2,1,0:T(8,128)S(1)}, f32[1,640,128]{2,1,0:T(8,128)}, u32[]{:S(2)}) copy-start(f32[1,640,128]{2,1,0:T(8,128)} %param.15) | copy-start | bytes 983044

commit v3 on v2

--- a/solution.py
+++ b/solution.py
@@ -18,6 +18,7 @@
 PAD = 24
 WIDE = 128
 CHUNK = 256
+STRIP = 64
 MESH = pl.DeviceIdType.MESH
 F32 = jnp.float32
 BF16 = jnp.bfloat16
@@ -41,37 +42,39 @@
 
 
 class Exchange:
-    def __init__(self, group, sems, row, src_of, dst_of):
+    def __init__(self, group, sems, row, src_of, dst_of, all_ref):
         self.group, self.sems, self.row = group, sems, row
-        self.src_of, self.dst_of = src_of, dst_of
-
-    def copy(self, peer, slot):
+        self.src_of, self.dst_of, self.all_ref = src_of, dst_of, all_ref
+
+    def copy(self, src, dst, peer):
         return pltpu.make_async_remote_copy(
-            src_ref=self.src_of(peer),
-            dst_ref=self.dst_of(slot),
-            send_sem=self.sems.at[2 * self.row, peer],
-            recv_sem=self.sems.at[2 * self.row + 1, slot],
+            src_ref=src,
+            dst_ref=dst,
+            send_sem=self.sems.at[2 * self.row],
+            recv_sem=self.sems.at[2 * self.row + 1],
             device_id=self.group.device(peer),
             device_id_type=MESH,
         )
 
-    def each(self, act):
+    def start(self):
         group = self.group
 
         def step(k, carry):
-            act(lax.rem(group.me + k, group.count))
+            peer = lax.rem(group.me + k, group.count)
+            self.copy(self.src_of(peer), self.dst_of(group.me), peer).start()
             return carry
 
         lax.fori_loop(1, group.count, step, 0)
 
-    def start(self):
-        self.each(lambda peer: self.copy(peer, self.group.me).start())
+    def whole(self):
+        peer = lax.rem(self.group.me + 1, self.group.count)
+        return self.copy(self.all_ref, self.all_ref, peer)
 
     def wait_recv(self):
-        self.each(lambda peer: self.copy(peer, peer).wait_recv())
+        self.whole().wait_recv()
 
     def wait_send(self):
-        self.each(lambda peer: self.copy(peer, peer).wait_send())
+        self.whole().wait_send()
 
 
 def meet(*groups):
@@ -176,6 +179,10 @@
     "b", "obs", "l0", "traj", "w_in", "w_out", "modes", "base", "scale", "limit", "ocol", "count",
     "vrow",
 )
+LOADS = {
+    "l0": "l0", "traj": "traj", "b": "b", "modes": "fmod", "obs": "obs", "base": "base",
+    "scale": "scale", "limit": "limit", "ocol": "ocol", "count": "count", "vrow": "vrow",
+}
 OUTPUTS = ("mult", "obs_a", "obs_b", "incr_a", "incr_b")
 NAMES = (
     "shift", "vpair", "vz", "vcore", "hl", "hb", "hr", "nfw", "mret", "sret", "mful", "efw",
@@ -202,7 +209,7 @@
         "ht": ((width, deep), F32), "qt": ((width, deep), F32),
         "cl": ((GRPS, PAD, 2 * KW), F32),
         "thi": ((total_cols, 2 * KW), BF16), "tlo": ((total_cols, 2 * KW), BF16),
-        "spec": ((PAD, 2 * KW), F32), "var": ((64, 1), F32), "fmod": ((deep // GRPS, deep), F32),
+        "spec": ((PAD, 2 * KW), F32), "var": ((64, 1), F32),
         "pick": ((width, 64), BF16), "pick_t": ((64, width), BF16),
         "r1": (field, F32), "p3": (field, F32), "q": (field, F32),
         "rb1": ((RING, 8, WIDE), F32), "rb2": ((COLN, 8, WIDE), F32),
@@ -212,6 +219,15 @@
         out[name] = (field, F32)
     for name in ("nt", "mt", "bt", "sbt", "l0t", "r1t", "et", "m2t", "t1t", "qst"):
         out[name] = (every, F32)
+    loaded = {
+        "b": (field, F32), "obs": ((64, deep), F32), "l0": (field, F32),
+        "traj": ((deep, width), BF16), "fmod": ((deep // GRPS, deep), F32),
+        "base": ((2 * WIDE + 2 * COLN, KW), F32), "scale": ((deep // WIDE, WIDE), F32),
+        "limit": ((deep // WIDE, WIDE), jnp.int32), "ocol": ((1, 64), jnp.int32),
+        "count": ((1, 1), jnp.int32), "vrow": ((1, 64), F32),
+    }
+    for name, kind in loaded.items():
+        out["in_" + name] = kind
     for i in range(3):
         out[f"am{i}"] = (amps, F32)
         out[f"cb{i}"] = (flat, F32)
@@ -223,7 +239,11 @@
 
 
 def kernel(names, *refs):
-    x = types.SimpleNamespace(**dict(zip(names, refs)))
+    given = dict(zip(names, refs))
+    loads = {n: (given[n], given["in_" + to]) for n, to in LOADS.items()}
+    x = types.SimpleNamespace(**given)
+    for n, to in LOADS.items():
+        setattr(x, to, given["in_" + to])
     s, c, g = lax.axis_index("sub"), lax.axis_index("col"), lax.axis_index("grp")
     core, z = lax.rem(c, CORES), lax.div(c, CORES)
     r = s * GRPS + g
@@ -235,42 +255,51 @@
     same = Group(z, COLN // CORES, lambda p: {"col": p * CORES + core})
     chip = Group(core, CORES, lambda p: {"col": z * CORES + p})
 
-    def over(name, group, src, dst):
-        return Exchange(group, x.sems, NAMES.index(name), src, dst)
+    def over(name, group, src, dst, all_ref):
+        return Exchange(group, x.sems, NAMES.index(name), src, dst, all_ref)
+
+    def others(ref, group):
+        return ref.at[pl.ds(0, group.count - 1)]
 
     def next_sub(p):
         return lax.rem(lax.div(p, GRPS) + 1, SUBS)
 
     def forward(name, src, dst):
-        return over(name, ring, lambda p: src.at[p], lambda i: dst.at[i])
+        return over(name, ring, lambda p: src.at[p], lambda i: dst.at[i], others(dst, ring))
 
     def giving(name, src, dst):
-        return over(name, ring, lambda p: src.at[lax.div(p, GRPS)], lambda i: dst.at[i])
+        at = others(dst, ring)
+        return over(name, ring, lambda p: src.at[lax.div(p, GRPS)], lambda i: dst.at[i], at)
 
     def giving_next(name, src, dst):
-        return over(name, ring, lambda p: src.at[next_sub(p)], lambda i: dst.at[i])
+        return over(name, ring, lambda p: src.at[next_sub(p)], lambda i: dst.at[i], others(dst, ring))
 
     def halves(name, src, dst):
-        return over(name, subs, lambda p: src.at[p * GRPS + g], lambda i: dst.at[i])
+        at = others(dst, subs)
+        return over(name, subs, lambda p: src.at[p * GRPS + g], lambda i: dst.at[i], at)
 
     def amps(name, src, dst):
-        return over(name, cols, lambda p: src.at[p], lambda i: dst.at[:, lanes(i)])
+        at = dst.at[:, pl.ds(0, (COLN - 1) * WIDE)]
+        return over(name, cols, lambda p: src.at[p], lambda i: dst.at[:, lanes(i)], at)
 
     def backs(name, src, dst):
-        return over(name, cols, lambda p: src.at[:, :, lanes(p)], lambda i: dst.at[i])
+        at = others(dst, cols)
+        return over(name, cols, lambda p: src.at[:, :, lanes(p)], lambda i: dst.at[i], at)
 
     def gathers(name, buf):
-        return over(name, ring, lambda p: buf.at[r], lambda i: buf.at[i])
+        return over(name, ring, lambda p: buf.at[r], lambda i: buf.at[i], others(buf, ring))
 
     row = NAMES.index("shift")
     shift = pltpu.make_async_remote_copy(
-        src_ref=x.l0, dst_ref=x.lup, send_sem=x.sems.at[2 * row, 0],
-        recv_sem=x.sems.at[2 * row + 1, 0],
+        src_ref=x.l0, dst_ref=x.lup, send_sem=x.sems.at[2 * row],
+        recv_sem=x.sems.at[2 * row + 1],
         device_id={"sub": lax.rem(s + SUBS - 1, SUBS)}, device_id_type=MESH,
     )
-    vpair = over("vpair", pair, lambda p: x.vpad.at[c], lambda i: x.voth.at[z, core])
-    vz = over("vz", same, lambda p: x.voth.at[z, core], lambda i: x.voth.at[i, core])
-    vcore = over("vcore", chip, lambda p: x.voth.at[:, core], lambda i: x.voth.at[:, i])
+    vpair = over("vpair", pair, lambda p: x.vpad.at[c], lambda i: x.voth.at[z, core], x.voth.at[z, core])
+    at = x.voth.at[pl.ds(0, same.count - 1), core]
+    vz = over("vz", same, lambda p: x.voth.at[z, core], lambda i: x.voth.at[i, core], at)
+    at = x.voth.at[:, 1 - core]
+    vcore = over("vcore", chip, lambda p: x.voth.at[:, core], lambda i: x.voth.at[:, i], at)
     hl = halves("hl", x.l0, x.l0t)
     hb = halves("hb", x.b, x.bt)
     hr = halves("hr", x.r1, x.r1t)
@@ -287,22 +316,36 @@
     ufw = forward("ufw", x.up, x.ubuf)
     gat1, gat2 = gathers("gat1", x.gb1), gathers("gat2", x.gb2)
     red1 = gathers("red1", x.rb1)
-    red2 = over("red2", cols, lambda p: x.rb2.at[c], lambda i: x.rb2.at[i])
+    red2 = over("red2", cols, lambda p: x.rb2.at[c], lambda i: x.rb2.at[i], others(x.rb2, cols))
     amp0, amp1, amp2 = (amps(f"amp{i}", getattr(x, f"am{i}"), getattr(x, f"cb{i}")) for i in range(3))
     lba, bak1, bak2 = (
         backs(n, getattr(x, f"wd{i}"), getattr(x, f"bk{i}"))
         for i, n in enumerate(("lba", "bak1", "bak2"))
     )
-    clx = over("clx", pair, lambda p: x.cl.at[g], lambda i: x.cl.at[i])
+    clx = over("clx", pair, lambda p: x.cl.at[g], lambda i: x.cl.at[i], x.cl.at[1 - g])
     sent = [vpair, vz, vcore, hl, hb, hr, nfw, mret, sret, mful, efw, m2ret, tfw, qret, m2ful,
             afw, ufw, gat1, gat2, red1, red2, amp0, amp1, amp2, lba, bak1, bak2, clx]
 
-    get_in = pltpu.make_async_copy(x.w_in, x.fin, x.local.at[0])
-    get_out = pltpu.make_async_copy(x.w_out, x.fout, x.local.at[1])
-    get_in.start()
-    get_modes = pltpu.make_async_copy(x.modes, x.fmod, x.local.at[2])
-    get_out.start()
-    get_modes.start()
+    strips = deep // STRIP
+
+    def get_in(j):
+        return pltpu.make_async_copy(x.w_in.at[chunk(j), :], x.fin.at[chunk(j), :], x.local.at[j])
+
+    def get_out(j):
+        at = chunk(j, STRIP)
+        return pltpu.make_async_copy(x.w_out.at[at, :], x.fout.at[at, :], x.local.at[hidden // CHUNK + j])
+
+    load = {
+        n: pltpu.make_async_copy(*loads[n], x.local.at[hidden // CHUNK + strips + i]) for i, n in enumerate(loads)
+    }
+    for n in ("l0", "traj", "b"):
+        load[n].start()
+    for j in range(hidden // CHUNK):
+        get_in(j).start()
+    for j in range(strips):
+        get_out(j).start()
+    for n in tuple(load)[3:]:
+        load[n].start()
 
     def first_half(columns):
         weights = (x.woh, x.wol) if columns else (x.wih, x.wil)
@@ -393,18 +436,21 @@
     has_later = jnp.where(s < SUBS - 1, 1.0, 0.0)
     leads = jnp.where(g == 0, 1.0, 0.0)
 
-    owned = x.modes.shape[0] // COLN
+    owned = x.fmod.shape[0] // COLN
     meet(ring, cols)
+    load["l0"].wait()
+    load["traj"].wait()
     traj_t = x.traj[...].astype(F32).T
     x.zz[:width] = traj_t.astype(BF16)
     met(ring, cols)
     shift.start()
+    load["b"].wait()
     hb.start()
     x.bt[s] = x.b[r]
     x.l0t[s] = x.l0[r]
-    get_in.wait()
 
     def open_in(j, carry):
+        get_in(j).wait()
         high, low = split(x.fin[chunk(j), :])
         x.wih[chunk(j), :] = high
         x.wil[chunk(j), :] = low
@@ -413,20 +459,22 @@
         return carry
 
     lax.fori_loop(0, hidden // CHUNK, open_in, 0)
-    get_out.wait()
 
     def open_out(j, carry):
-        high, low = split(x.fout[chunk(j, 64), :])
-        x.woh[chunk(j, 64), :] = high
-        x.wol[chunk(j, 64), :] = low
+        get_out(j).wait()
+        at = chunk(j, STRIP)
+        high, low = split(x.fout[at, :])
+        x.woh[at, :] = high
+        x.wol[at, :] = low
         return carry
 
-    lax.fori_loop(0, deep // 64, open_out, 0)
+    lax.fori_loop(0, strips, open_out, 0)
     shift.wait_recv()
     put(x.np_, adjoint(whole(x.lup).T) * has_later)
     nfw.start()
     x.nbuf[r] = x.np_[r]
-    get_modes.wait()
+    for n in tuple(load)[3:]:
+        load[n].wait()
     for i in range(COLN):
         x.vpad[i, :owned] = x.fmod[i * owned:(i + 1) * owned]
         x.vpad[i, owned:] = jnp.zeros((PAD - owned, deep), F32)
@@ -657,12 +705,15 @@
     move, obs_a, obs_b, incr_a, incr_b = pl.pallas_call(
         lambda *refs: kernel(names, *refs),
         name="saddle",
-        out_shape=[jax.ShapeDtypeStruct(shape, F32) for shape in shapes],
-        in_specs=[away if n in ("w_in", "w_out", "modes") else vmem for n in INPUTS],
+        out_shape=[pltpu.VMEM(shape, F32) for shape in shapes],
+        in_specs=[away] * len(INPUTS),
         out_specs=[vmem] * len(shapes),
         scratch_shapes=[pltpu.VMEM(*scratch[n]) for n in scratch]
-        + [pltpu.SemaphoreType.DMA((3,)), pltpu.SemaphoreType.DMA((2 * len(NAMES), 16))],
-        compiler_params=pltpu.CompilerParams(collective_id=0, has_side_effects=True),
+        + [
+            pltpu.SemaphoreType.DMA((hidden // CHUNK + deep // STRIP + len(LOADS),)),
+            pltpu.SemaphoreType.DMA((2 * len(NAMES),)),
+        ],
+        compiler_params=pltpu.CompilerParams(collective_id=0, has_side_effects=True, vmem_limit_bytes=59_000_000),
     )(*(args[n] for n in INPUTS))
     mult = start_mult + move.reshape(1, deep, width)
     incr = incr_a + incr_b

time: 144 us -> 127 us (0.88)
  Pallas kernels: 137 us -> 123 us
  other arithmetic: 5.24 us -> 2.2 us
    pallas_call x1, Pallas kernels: 137 us -> 123 us  [on_device(): pl.pallas_call(lambda *refs: kernel(names, *refs), name='saddle', out_sha...]
where the time goes in v3:
time: 127 us; the launch traced here: 126 us
  Pallas kernels  123 us (97%)
  other arithmetic  2.2 us (2%)
  between operations  1.31 us (1%)
    pallas_call x1, Pallas kernels, on_device(): pl.pallas_call(lambda *refs: kernel(names, *refs), name='saddle', out_sha...  123 us

profile of v3, /device:TPU:1, one launch (start us, length us, event | category | flops | bytes accessed | tf_op | source)
XLA Modules:
  0.0 126.4 jit_solution(746976264355851350)
XLA Ops:
  1.3 0.0 copy-start
  1.3 122.9 %saddle.1 = (f32[16,40,128]{2,1,0:T(8,128)S(1)}, f32[64,640]{1,0:T(8,128)S(1)}, f32[64,640]{1,0:T(8,128)S(1)}, f32[16,40,128]{2,1,0:T(8,128)S(1)}, f32[16,40,128]{2,1,0:T(8,128)S(1)}) custom-call(f32[16,40,128]{2,1,0:T(8,128)} %bitcast.14, f32[64,640]{1,0:T(8,128)} %bitcast.16, f32[16,40,128]{2,1,0:T(8,128)} %bitcast.13, bf16[640,128]{1,0:T(8,128)(2,1)} %bitcast.17, ...), custom_call_target="tpu_custom_call" | custom-call | tf_op jit(solution)/shard_map/saddle/pallas_call | solution.py:705
  124.2 0.0 copy-done
  124.2 0.8 bitcast_add_fusion
  125.0 0.7 subtract_bitcast_fusion
  125.7 0.8 add.7
Async XLA Ops:
  1.3 122.9 %copy-start = (f32[1,640,128]{2,1,0:T(8,128)S(1)}, f32[1,640,128]{2,1,0:T(8,128)}, u32[]{:S(2)}) copy-start(f32[1,640,128]{2,1,0:T(8,128)} %param.15) | copy-start | bytes 983044

commit v4 on v3

--- a/solution.py
+++ b/solution.py
@@ -126,32 +126,36 @@
     return value[:rows] + value[rows:] + mm(both[:rows], b[1], dims)
 
 
-def pair_sums(buffer, into):
+ALL = slice(None)
+PARTS = (slice(0, 24), slice(24, 40))
+
+
+def pair_sums(buffer, into, rows=ALL):
     for t in range(SUBS):
-        into[t] = buffer[2 * t] + buffer[2 * t + 1]
-
-
-def suffix_sums(rows, into):
-    total = rows[SUBS - 1]
-    into[SUBS - 1] = total
+        into[t, rows] = buffer[2 * t, rows] + buffer[2 * t + 1, rows]
+
+
+def suffix_sums(terms, into, rows=ALL):
+    total = terms[SUBS - 1, rows]
+    into[SUBS - 1, rows] = total
     for t in range(SUBS - 2, -1, -1):
-        total = total + rows[t]
-        into[t] = total
-
-
-def prefix_sums(rows, into):
-    total = rows[0]
+        total = total + terms[t, rows]
+        into[t, rows] = total
+
+
+def prefix_sums(terms, into):
+    total = terms[0]
     into[0] = total
     for t in range(1, SUBS):
-        total = total + rows[t]
+        total = total + terms[t]
         into[t] = total
 
 
-def lagged_sums(rows, into):
-    total = jnp.zeros_like(rows[0])
+def lagged_sums(terms, into, rows=ALL):
+    total = jnp.zeros_like(terms[0, rows])
     for t in range(SUBS):
-        into[t] = total
-        total = total + rows[t]
+        into[t, rows] = total
+        total = total + terms[t, rows]
 
 
 def fold(x):
@@ -187,7 +191,7 @@
 NAMES = (
     "shift", "vpair", "vz", "vcore", "hl", "hb", "hr", "nfw", "mret", "sret", "mful", "efw",
     "m2ret", "tfw", "qret", "m2ful", "afw", "ufw", "gat1", "gat2", "red1", "amp0", "lba", "amp1",
-    "bak1", "amp2", "bak2", "red2", "clx",
+    "bak1", "amp2", "bak2", "red2", "clx", "nfw1", "mret1", "tfw1", "qret1", "efw1", "m2ret1",
 )
 
 
@@ -264,15 +268,19 @@
     def next_sub(p):
         return lax.rem(lax.div(p, GRPS) + 1, SUBS)
 
-    def forward(name, src, dst):
-        return over(name, ring, lambda p: src.at[p], lambda i: dst.at[i], others(dst, ring))
-
-    def giving(name, src, dst):
-        at = others(dst, ring)
-        return over(name, ring, lambda p: src.at[lax.div(p, GRPS)], lambda i: dst.at[i], at)
-
-    def giving_next(name, src, dst):
-        return over(name, ring, lambda p: src.at[next_sub(p)], lambda i: dst.at[i], others(dst, ring))
+    def forward(name, src, dst, rows=slice(0, deep // RING)):
+        at = dst.at[pl.ds(0, RING - 1), rows]
+        return over(name, ring, lambda p: src.at[p, rows], lambda i: dst.at[i, rows], at)
+
+    def giving(name, src, dst, rows=slice(0, deep // RING)):
+        at = dst.at[pl.ds(0, RING - 1), rows]
+        return over(
+            name, ring, lambda p: src.at[lax.div(p, GRPS), rows], lambda i: dst.at[i, rows], at
+        )
+
+    def giving_next(name, src, dst, rows=slice(0, deep // RING)):
+        at = dst.at[pl.ds(0, RING - 1), rows]
+        return over(name, ring, lambda p: src.at[next_sub(p), rows], lambda i: dst.at[i, rows], at)
 
     def halves(name, src, dst):
         at = others(dst, subs)
@@ -288,6 +296,9 @@
 
     def gathers(name, buf):
         return over(name, ring, lambda p: buf.at[r], lambda i: buf.at[i], others(buf, ring))
+
+    def both(kind, name, src, dst):
+        return [kind(n, src, dst, rows) for n, rows in zip((name, name + "1"), PARTS)]
 
     row = NAMES.index("shift")
     shift = pltpu.make_async_remote_copy(
@@ -303,14 +314,14 @@
     hl = halves("hl", x.l0, x.l0t)
     hb = halves("hb", x.b, x.bt)
     hr = halves("hr", x.r1, x.r1t)
-    nfw = forward("nfw", x.np_, x.nbuf)
-    mret = giving_next("mret", x.mt, x.mup)
+    nfw = both(forward, "nfw", x.np_, x.nbuf)
+    mret = both(giving_next, "mret", x.mt, x.mup)
     sret = giving("sret", x.sbt, x.sb)
     mful = giving("mful", x.mt, x.mfull)
-    efw = forward("efw", x.ep, x.ebuf)
-    m2ret = giving_next("m2ret", x.m2t, x.m2up)
-    tfw = forward("tfw", x.tp, x.tbuf)
-    qret = giving("qret", x.qst, x.qs)
+    efw = both(forward, "efw", x.ep, x.ebuf)
+    m2ret = both(giving_next, "m2ret", x.m2t, x.m2up)
+    tfw = both(forward, "tfw", x.tp, x.tbuf)
+    qret = both(giving, "qret", x.qst, x.qs)
     m2ful = giving("m2ful", x.m2t, x.m2full)
     afw = forward("afw", x.ap, x.abuf)
     ufw = forward("ufw", x.up, x.ubuf)
@@ -323,8 +334,8 @@
         for i, n in enumerate(("lba", "bak1", "bak2"))
     )
     clx = over("clx", pair, lambda p: x.cl.at[g], lambda i: x.cl.at[i], x.cl.at[1 - g])
-    sent = [vpair, vz, vcore, hl, hb, hr, nfw, mret, sret, mful, efw, m2ret, tfw, qret, m2ful,
-            afw, ufw, gat1, gat2, red1, red2, amp0, amp1, amp2, lba, bak1, bak2, clx]
+    sent = [vpair, vz, vcore, hl, hb, hr, *nfw, *mret, sret, mful, *efw, *m2ret, *tfw, *qret,
+            m2ful, afw, ufw, gat1, gat2, red1, red2, amp0, amp1, amp2, lba, bak1, bak2, clx]
 
     strips = deep // STRIP
 
@@ -471,7 +482,8 @@
     lax.fori_loop(0, strips, open_out, 0)
     shift.wait_recv()
     put(x.np_, adjoint(whole(x.lup).T) * has_later)
-    nfw.start()
+    for part in nfw:
+        part.start()
     x.nbuf[r] = x.np_[r]
     for n in tuple(load)[3:]:
         load[n].wait()
@@ -530,10 +542,11 @@
     vpair.wait_recv()
     vz.start()
     x.ht[...] = spread_rows(x.obs[...] / x.var[...])
-    nfw.wait_recv()
-    pair_sums(x.nbuf, x.nt)
-    suffix_sums(x.nt, x.mt)
-    mret.start()
+    for rows, come, go in zip(PARTS, nfw, mret):
+        come.wait_recv()
+        pair_sums(x.nbuf, x.nt, rows)
+        suffix_sums(x.nt, x.mt, rows)
+        go.start()
     x.mup[r] = x.mt[lax.rem(s + 1, SUBS)]
     hb.wait_recv()
     prefix_sums(x.bt, x.sbt)
@@ -543,7 +556,8 @@
     x.mfull[r] = x.mt[s]
     amp0.wait_recv()
     x.cl[g] = coefficients(x.cb0)
-    mret.wait_recv()
+    for part in mret:
+        part.wait_recv()
     amplitudes(x.mup, x.am1)
     amp1.start()
     clx.start()
@@ -554,7 +568,8 @@
     amp1.wait_recv()
     x.gb1[r] = coefficients(x.cb1)
     gat1.start()
-    efw.start()
+    for part in efw:
+        part.start()
     x.ebuf[r] = x.ep[r]
     clx.wait_recv()
     spread_back(x.cl[...].reshape(GRPS * PAD, 2 * KW), x.wd0)
@@ -566,14 +581,16 @@
     spread_back(summed(x.gb1), x.wd1)
     bak1.start()
     x.bk1[c] = x.wd1[:, :, lanes(c)]
-    efw.wait_recv()
-    pair_sums(x.ebuf, x.et)
-    suffix_sums(x.et, x.m2t)
-    m2ret.start()
+    for rows, come, go in zip(PARTS, efw, m2ret):
+        come.wait_recv()
+        pair_sums(x.ebuf, x.et, rows)
+        suffix_sums(x.et, x.m2t, rows)
+        go.start()
     m2ful.start()
     x.m2full[r] = x.m2t[s]
     x.m2up[r] = x.m2t[lax.rem(s + 1, SUBS)]
-    m2ret.wait_recv()
+    for part in m2ret:
+        part.wait_recv()
     amplitudes(x.m2up, x.am2)
     amp2.start()
     lba.start()
@@ -590,7 +607,8 @@
         gat2.start()
 
     put(x.tp, tangent(p3t, between))
-    tfw.start()
+    for part in tfw:
+        part.start()
     x.tbuf[r] = x.tp[r]
     gat2.wait_recv()
     spread_back(summed(x.gb2), x.wd2)
@@ -598,10 +616,11 @@
     x.bk2[c] = x.wd2[:, :, lanes(c)]
     put(x.p3, x.p3t[...])
     x.seen[...] = pick_rows(x.p3t[...])
-    tfw.wait_recv()
-    pair_sums(x.tbuf, x.t1t)
-    lagged_sums(x.t1t, x.qst)
-    qret.start()
+    for rows, come, go in zip(PARTS, tfw, qret):
+        come.wait_recv()
+        pair_sums(x.tbuf, x.t1t, rows)
+        lagged_sums(x.t1t, x.qst, rows)
+        go.start()
     x.qs[r] = x.qst[s]
     a2 = adjoint(whole(x.m2up).T) * has_later
     put(x.ap, a2 + leads * spread_rows(x.seen[...] / x.var[...]))
@@ -612,7 +631,8 @@
     hr.start()
     hl.start()
     x.r1t[s] = x.r1[r]
-    qret.wait_recv()
+    for part in qret:
+        part.wait_recv()
     bak2.wait_recv()
     qt = whole(x.qs).T - restored_t(x.bk2)
     x.qt[...] = qt

time: 127 us -> 128 us (level)
  Pallas kernels: 123 us -> 125 us
    pallas_call x1, Pallas kernels: 123 us -> 125 us  [on_device(): pl.pallas_call(lambda *refs: kernel(names, *refs), name='saddle', out_sha...]
where the time goes in v4:
time: 128 us
  Pallas kernels  125 us (98%)
  other arithmetic  2.2 us (2%)
  between operations  1.31 us (1%)
    pallas_call x1, Pallas kernels, on_device(): pl.pallas_call(lambda *refs: kernel(names, *refs), name='saddle', out_sha...  125 us

profile of v4, /device:TPU:1, one launch (start us, length us, event | category | flops | bytes accessed | tf_op | source)
XLA Modules:
  0.0 128.1 jit_solution(1594352454480148309)
XLA Ops:
  1.3 0.0 copy-start
  1.3 124.6 %saddle.1 = (f32[16,40,128]{2,1,0:T(8,128)S(1)}, f32[64,640]{1,0:T(8,128)S(1)}, f32[64,640]{1,0:T(8,128)S(1)}, f32[16,40,128]{2,1,0:T(8,128)S(1)}, f32[16,40,128]{2,1,0:T(8,128)S(1)}) custom-call(f32[16,40,128]{2,1,0:T(8,128)} %bitcast.14, f32[64,640]{1,0:T(8,128)} %bitcast.16, f32[16,40,128]{2,1,0:T(8,128)} %bitcast.13, bf16[640,128]{1,0:T(8,128)(2,1)} %bitcast.17, ...), custom_call_target="tpu_custom_call" | custom-call | tf_op jit(solution)/shard_map/saddle/pallas_call | solution.py:725
  125.9 0.0 copy-done
  125.9 0.8 bitcast_add_fusion
  126.7 0.7 subtract_bitcast_fusion
  127.4 0.8 add.7
Async XLA Ops:
  1.3 124.6 %copy-start = (f32[1,640,128]{2,1,0:T(8,128)S(1)}, f32[1,640,128]{2,1,0:T(8,128)}, u32[]{:S(2)}) copy-start(f32[1,640,128]{2,1,0:T(8,128)} %param.15) | copy-start | bytes 983044
